TPU v7x, 16 devices: a whole 2x2x2 slice. The times are simulated.
16 devices in a mesh: replica: 4 (over z, y), pool: 4 (over x, core).
Axes of the slice: x: 2, y: 2, z: 2, core: 2. Of those that a mesh axis runs over, the one named last changes fastest.
Arguments:
- pool: bfloat16 [2, 256, 2, 256, 8, 128], P(None, ('replica', 'pool')), parts along dimension 1
- page_idx: int32 [4, 16, 8], P(None, ('replica', 'pool')), parts along dimension 1
- count: int32 [16, 4], P(('replica', 'pool')), parts along dimension 0
- x: bfloat16 [16, 128, 3072], P(('replica', 'pool')), parts along dimension 0
- norm_attn: bfloat16 [2, 3072], replicated
- wq: bfloat16 [2, 3072, 3072], replicated
- wk: bfloat16 [2, 3072, 1024], replicated
- wv: bfloat16 [2, 3072, 1024], replicated
- wo: bfloat16 [2, 3072, 3072], replicated
- norm_mlp: bfloat16 [2, 3072], replicated
- w_gate: bfloat16 [2, 3072, 8192], replicated
- w_up: bfloat16 [2, 3072, 8192], replicated
- w_down: bfloat16 [2, 8192, 3072], replicated
Outputs:
- output: bfloat16 [16, 128, 3072], P(('replica', 'pool')), parts along dimension 0
There are 4 independent parts. A program takes and returns all parts, laid end to end along the dimension named above; an argument that names none is the same for every part.
All inputs are finite; a program needn't handle non-finite values.
Results may differ from a plain program's by a relative error of at most 0.0156318.
Values are sent between devices in bfloat16 or wider.
A program may use at most 1.75 GiB of HBM per device.

v0:
```python
import jax
import jax.numpy as jnp
from jax import lax
from jax.sharding import PartitionSpec as P

EPS = 1e-5
ROPE_BASE = 500000.0


def rms_norm(vals, gain):
    vals_f = vals.astype(jnp.float32)
    inv_rms = lax.rsqrt(jnp.mean(vals_f * vals_f, axis=-1, keepdims=True) + EPS)
    return (vals_f * inv_rms * gain.astype(jnp.float32)).astype(jnp.bfloat16)


def rotate(proj, tokens):
    half = proj.shape[-1] // 2
    freqs = ROPE_BASE ** (-jnp.arange(half, dtype=jnp.float32) / half)
    angles = jnp.arange(tokens, dtype=jnp.float32)[:, None] * freqs[None, :]
    cos_t = jnp.cos(angles)[:, None, :]
    sin_t = jnp.sin(angles)[:, None, :]
    first = proj[..., :half]
    second = proj[..., half:]
    return jnp.concatenate([first * cos_t - second * sin_t, second * cos_t + first * sin_t], axis=-1)


def decoder_layer(x_req, incoming, pre_ok, causal, weights):
    g_attn, wq_l, wk_l, wv_l, wo_l, g_mlp, wg_l, wu_l, wd_l = weights
    tokens = x_req.shape[0]
    kv_heads, head_dim = incoming.shape[4], incoming.shape[5]
    heads = wq_l.shape[1] // head_dim
    scale = head_dim ** -0.5
    h_attn = rms_norm(x_req, g_attn)
    q_proj = jnp.dot(h_attn, wq_l, preferred_element_type=jnp.float32).reshape(tokens, heads, head_dim)
    k_proj = jnp.dot(h_attn, wk_l, preferred_element_type=jnp.float32).reshape(tokens, kv_heads, head_dim)
    q_group = rotate(q_proj, tokens).astype(jnp.bfloat16).reshape(tokens, kv_heads, heads // kv_heads, head_dim)
    k_new = rotate(k_proj, tokens).astype(jnp.bfloat16)
    v_new = jnp.dot(h_attn, wv_l, preferred_element_type=jnp.float32).astype(jnp.bfloat16).reshape(tokens, kv_heads, head_dim)
    k_pre = incoming[:, :, 0]
    v_pre = incoming[:, :, 1]
    score_pre = jnp.einsum('tgrd,oksgd->grtoks', q_group, k_pre, preferred_element_type=jnp.float32) * scale
    score_pre = jnp.where(pre_ok, score_pre, -1e30)
    score_new = jnp.einsum('tgrd,ugd->grtu', q_group, k_new, preferred_element_type=jnp.float32) * scale
    score_new = jnp.where(causal, score_new, -1e30)
    peak = jnp.maximum(jnp.max(score_pre, axis=(3, 4, 5)), jnp.max(score_new, axis=3))
    exp_pre = jnp.exp(score_pre - peak[:, :, :, None, None, None])
    exp_new = jnp.exp(score_new - peak[:, :, :, None])
    inv_total = 1.0 / (jnp.sum(exp_pre, axis=(3, 4, 5)) + jnp.sum(exp_new, axis=3))
    prob_pre = (exp_pre * inv_total[:, :, :, None, None, None]).astype(jnp.bfloat16)
    prob_new = (exp_new * inv_total[:, :, :, None]).astype(jnp.bfloat16)
    attn_sum = jnp.einsum('grtoks,oksgd->tgrd', prob_pre, v_pre, preferred_element_type=jnp.float32) + jnp.einsum('grtu,ugd->tgrd', prob_new, v_new, preferred_element_type=jnp.float32)
    attn = attn_sum.astype(jnp.bfloat16).reshape(tokens, heads * head_dim)
    x_mid = (x_req.astype(jnp.float32) + jnp.dot(attn, wo_l, preferred_element_type=jnp.float32)).astype(jnp.bfloat16)
    h_mlp = rms_norm(x_mid, g_mlp)
    gate = jnp.dot(h_mlp, wg_l, preferred_element_type=jnp.float32)
    up_proj = jnp.dot(h_mlp, wu_l, preferred_element_type=jnp.float32)
    gated = (jax.nn.silu(gate) * up_proj).astype(jnp.bfloat16)
    return (x_mid.astype(jnp.float32) + jnp.dot(gated, wd_l, preferred_element_type=jnp.float32)).astype(jnp.bfloat16)


def solution(mesh):
    group = mesh.shape['pool']
    by_request = P(('replica', 'pool'))
    by_owner = P(None, ('replica', 'pool'))
    shared = P()

    def per_device(pool_loc, idx_loc, count_loc, x_loc, norm_attn, wq, wk, wv, wo, norm_mlp, w_gate, w_up, w_down):
        layers = pool_loc.shape[0]
        page_len, kv_heads, head_dim = pool_loc.shape[3], pool_loc.shape[4], pool_loc.shape[5]
        slots = idx_loc.shape[2]
        tokens = x_loc.shape[1]
        send_rows = idx_loc.reshape(group * slots)
        slot_ok = jnp.arange(slots)[None, :] < count_loc[0][:, None]
        pre_ok = jnp.broadcast_to(slot_ok[:, :, None], (group, slots, page_len))
        causal = jnp.arange(tokens)[None, :] <= jnp.arange(tokens)[:, None]
        x_req = x_loc[0]
        for layer in range(layers):
            outgoing = jnp.take(pool_loc[layer], send_rows, axis=0).reshape(group, slots, 2, page_len, kv_heads, head_dim)
            incoming = lax.all_to_all(outgoing, 'pool', 0, 0, tiled=True)
            weights = (norm_attn[layer], wq[layer], wk[layer], wv[layer], wo[layer], norm_mlp[layer], w_gate[layer], w_up[layer], w_down[layer])
            x_req = decoder_layer(x_req, incoming, pre_ok, causal, weights)
        return x_req[None]

    return jax.shard_map(per_device, mesh=mesh, in_specs=(by_owner, by_owner, by_request, by_request, shared, shared, shared, shared, shared, shared, shared, shared, shared), out_specs=by_request, check_vma=False)
```

profile of v0, /device:TPU:0, one launch (start us, length us, event | category | flops | bytes accessed | tf_op | source)
XLA Modules:
  0.0 1183.0 jit_solution(7946883555966646024)
XLA Ops:
  2.0 22.6 %slice_bitcast_fusion.2 = (bf16[16,2,256,8,128]{4,3,2,1,0:T(8,128)(2,1)}, bf16[16,2,256,8,128]{4,3,2,1,0:T(8,128)(2,1)}) fusion(bf16[2,16,2,256,8,128]{5,4,3,2,1,0:T(8,128)(2,1)} %param.15), kind=kLoop, calls=%fused_computation.52 | loop fusion | bytes 67108864 | tf_op jit(solution)/shard_map/squeeze | solution.py:78
  43.4 18.9 %gather_fusion = bf16[32,2,256,8,128]{4,3,2,1,0:T(8,128)(2,1)} fusion(bf16[16,2,256,8,128]{4,3,2,1,0:T(8,128)(2,1)} %get-tuple-element.11, s32[1024]{0:T(1024)S(1)} %pad_clamp_fusion), kind=kCustom, calls=%fused_computation.clone | custom fusion | bytes 67108992 | tf_op jit(solution)/shard_map/jit(_take)/gather | solution.py:78
  62.4 44.3 %broadcast_select_fusion = (bf16[32,2,256,8,128]{4,3,2,1,0:T(8,128)(2,1)}, bf16[32,2,256,8,128]{4,3,2,1,0:T(8,128)(2,1)}) fusion(bf16[32,2,256,8,128]{4,3,2,1,0:T(8,128)(2,1)} %gather_fusion.1, pred[32]{0:T(512)(128)(4,1)S(1)} %compare_and_fusion, bf16[32,2,256,8,128]{4,3,2,1,0:T(8,128)(2,1)} %gather_fusion), kind=kLoop, calls=%fused_computation.36 | loop fusion | flops 33554432 | bytes 134217760 | tf_op jit(solution)/shard_map/jit(_take)/select_n | solution.py:78
  106.7 23.1 %copy.54 = bf16[4,8,2,256,8,128]{5,3,1,4,2,0:T(8,128)(2,1)} copy(bf16[4,8,2,256,8,128]{5,4,3,2,1,0:T(8,128)(2,1)} %bitcast.282) | data formatting | bytes 67108864 | tf_op jit(solution)/shard_map/reshape | solution.py:78
  139.5 24.9 %slice_bitcast_fusion = (bf16[3072,3072]{0,1:T(8,128)(2,1)}, bf16[3072,3072]{0,1:T(8,128)(2,1)}) fusion(bf16[2,3072,3072]{2,1,0:T(8,128)(2,1)} %param.20), kind=kLoop, calls=%fused_computation.43 | loop fusion | bytes 75497472 | tf_op jit(solution)/shard_map/dot_general | solution.py:34
  164.4 24.6 %copy.57 = bf16[3072,3072]{1,0:T(8,128)(2,1)} copy(bf16[3072,3072]{0,1:T(8,128)(2,1)} %get-tuple-element.7) | data formatting | bytes 37748736 | tf_op jit(solution)/shard_map/dot_general | solution.py:34
  208.2 23.2 %copy.65 = bf16[4,8,2,256,8,128]{5,3,1,4,2,0:T(8,128)(2,1)} copy(bf16[4,8,2,256,8,128]{5,4,3,2,1,0:T(8,128)(2,1)} %bitcast.281) | data formatting | bytes 67108864 | tf_op jit(solution)/shard_map/reshape | solution.py:78
  246.4 256.6 %all-to-all-done = bf16[4,8,2,256,8,128]{5,3,1,4,2,0:T(8,128)(2,1)} async-done(((bf16[4,8,2,256,8,128]{5,3,1,4,2,0:T(8,128)(2,1)}), bf16[4,8,2,256,8,128]{5,3,1,4,2,0:T(8,128)(2,1)}, u32[]{:S(2)}, u32[]{:S(2)}) %all-to-all-start) | async-done | bytes 33554464 | tf_op jit(solution)/shard_map/all_to_all | solution.py:79
  515.2 24.7 %copy.68 = bf16[3072,3072]{1,0:T(8,128)(2,1)} copy(bf16[3072,3072]{0,1:T(8,128)(2,1)} %get-tuple-element.6) | data formatting | bytes 37748736 | tf_op jit(solution)/shard_map/dot_general | solution.py:34
  550.1 23.2 %fusion.173 = (bf16[4,8,1,256,8,128]{5,3,1,4,2,0:T(8,128)(2,1)}, bf16[4,8,1,256,8,128]{5,3,1,4,2,0:T(8,128)(2,1)}) fusion(bf16[4,8,2,256,8,128]{5,3,1,4,2,0:T(8,128)(2,1)} %all-to-all-done), kind=kLoop, calls=%fused_computation.179 | loop fusion | bytes 67108864 | tf_op jit(solution)/shard_map/slice | solution.py:40
  573.3 21.6 %copy.100 = bf16[4,8,1,256,8,128]{3,5,0,1,4,2:T(8,128)(2,1)} copy(bf16[4,8,1,256,8,128]{5,3,1,4,2,0:T(8,128)(2,1)} %get-tuple-element.12) | data formatting | bytes 33554432
  594.9 40.9 %bitcast_reduce_fusion.1 = (f32[8,3,128]{2,1,0:T(4,128)S(1)}, f32[8,4,8,256,128,3]{4,3,5,2,1,0:T(8,128)}) fusion(pred[4,8]{1,0:T(4,128)(4,1)S(1)} %iota_compare_fusion.1, bf16[128,8,3,64]{3,0,2,1:T(8,128)(2,1)S(1)} %copy.59, bf16[128,8,3,64]{3,0,2,1:T(8,128)(2,1)S(1)} %copy.58, bf16[4,8,1,256,8,128]{5,3,1,4,2,0:T(8,128)(2,1)} %get-tuple-element.13), kind=kOutput, calls=%fused_computation.6 | convolution fusion | flops 6519518208 | bytes 118239264 | tf_op jit(solution)/shard_map/tgrd,oksgd->grtoks/dot_general | solution.py:41
  636.1 31.2 %fusion.2 = f32[8,3,128]{2,1,0:T(4,128)S(1)} fusion(f32[8,4,8,256,128,3]{4,3,5,2,1,0:T(8,128)} %get-tuple-element.33, f32[8,3,128]{2,1,0:T(4,128)S(1)} %max.22, pred[4,8]{1,0:T(4,128)(4,1)S(1)} %iota_compare_fusion.1), kind=kLoop, calls=%fused_computation.12 | loop fusion | flops 100660224 | bytes 100687904 | tf_op jit(solution)/shard_map/reduce_sum | solution.py:48
  667.3 46.8 %fusion.18 = f32[8,128,3,128,1,1]{3,1,5,4,2,0:T(8,128)} fusion(bf16[4,8,1,256,8,128]{3,5,0,1,4,2:T(8,128)(2,1)} %copy.100, f32[8,4,8,256,128,3]{4,3,5,2,1,0:T(8,128)} %get-tuple-element.33, f32[8,3,128]{2,1,0:T(4,128)S(1)} %add_divide_fusion.1, f32[8,3,128]{2,1,0:T(4,128)S(1)} %max.22, pred[4,8]{1,0:T(4,128)(4,1)S(1)} %iota_compare_fusion.1), kind=kOutput, calls=%fused_computation.28 | convolution fusion | flops 6568280064 | bytes 119037984 | tf_op jit(solution)/shard_map/grtoks,oksgd->tgrd/dot_general | solution.py:51
  726.3 149.2 %all-to-all-done.1 = bf16[4,8,2,256,8,128]{5,3,1,4,2,0:T(8,128)(2,1)} async-done(((bf16[4,8,2,256,8,128]{5,3,1,4,2,0:T(8,128)(2,1)}), bf16[4,8,2,256,8,128]{5,3,1,4,2,0:T(8,128)(2,1)}, u32[]{:S(2)}, u32[]{:S(2)}) %all-to-all-start.1) | async-done | bytes 33554464 | tf_op jit(solution)/shard_map/all_to_all | solution.py:79
  875.4 23.1 %fusion.172 = (bf16[4,8,1,256,8,128]{5,3,1,4,2,0:T(8,128)(2,1)}, bf16[4,8,1,256,8,128]{5,3,1,4,2,0:T(8,128)(2,1)}) fusion(bf16[4,8,2,256,8,128]{5,3,1,4,2,0:T(8,128)(2,1)} %all-to-all-done.1), kind=kLoop, calls=%fused_computation.178 | loop fusion | bytes 67108864 | tf_op jit(solution)/shard_map/slice | solution.py:40
  898.5 21.7 %copy.102 = bf16[4,8,1,256,8,128]{3,5,0,1,4,2:T(8,128)(2,1)} copy(bf16[4,8,1,256,8,128]{5,3,1,4,2,0:T(8,128)(2,1)} %get-tuple-element.8) | data formatting | bytes 33554432
  920.3 19.4 %fusion.16 = f32[128,8192]{1,0:T(8,128)} fusion(bf16[2,3072,8192]{2,1,0:T(8,128)(2,1)} %param.25, f32[128,3072]{1,0:T(8,128)S(1)} %copy-done.19, f32[3072]{0:T(1024)S(1)} %bitcast.301, f32[128]{0:T(128)S(1)} %add_rsqrt_fusion.2), kind=kOutput, calls=%fused_computation.26 | convolution fusion | flops 6443630592 | bytes 56111616 | tf_op jit(solution)/shard_map/dot_general | solution.py:55
  939.7 39.2 %multiply_reduce_fusion.1 = (f32[128]{0:T(128)S(1)}, f32[128,3072]{1,0:T(8,128)S(1)}) fusion(f32[128,3072]{1,0:T(8,128)} %get-tuple-element.37, bf16[2,8192,3072]{2,1,0:T(8,128)(2,1)} %param.27, bf16[2,3072,8192]{2,1,0:T(8,128)(2,1)} %param.26, f32[128,8192]{1,0:T(8,128)} %fusion.16, f32[3072]{0:T(1024)S(1)} %bitcast.302, f32[128]{0:T(128)S(1)} %add_rsqrt_fusion.2), kind=kOutput, calls=%fused_computation.105 | convolution fusion | flops 12894339072 | bytes 109589504 | tf_op jit(solution)/shard_map/dot_general | solution.py:58
  998.7 41.1 %bitcast_reduce_fusion = (f32[8,3,128]{2,1,0:T(4,128)S(1)}, f32[8,4,8,256,128,3]{4,3,5,2,1,0:T(8,128)}) fusion(pred[4,8]{1,0:T(4,128)(4,1)S(1)} %iota_compare_fusion.1, bf16[128,8,3,64]{3,0,2,1:T(8,128)(2,1)S(1)} %copy.70, bf16[128,8,3,64]{3,0,2,1:T(8,128)(2,1)S(1)} %copy.69, bf16[4,8,1,256,8,128]{5,3,1,4,2,0:T(8,128)(2,1)} %get-tuple-element.9), kind=kOutput, calls=%fused_computation.3 | convolution fusion | flops 6519518208 | bytes 118239264 | tf_op jit(solution)/shard_map/tgrd,oksgd->grtoks/dot_general | solution.py:41
  1040.7 31.2 %fusion.3 = f32[8,3,128]{2,1,0:T(4,128)S(1)} fusion(f32[8,4,8,256,128,3]{4,3,5,2,1,0:T(8,128)} %get-tuple-element.41, f32[8,3,128]{2,1,0:T(4,128)S(1)} %max.23, pred[4,8]{1,0:T(4,128)(4,1)S(1)} %iota_compare_fusion.1), kind=kLoop, calls=%fused_computation.13 | loop fusion | flops 100660224 | bytes 100687904 | tf_op jit(solution)/shard_map/reduce_sum | solution.py:48
  1072.3 45.3 %fusion.10 = f32[8,128,3,128,1,1]{3,1,5,4,2,0:T(8,128)S(1)} fusion(bf16[4,8,1,256,8,128]{3,5,0,1,4,2:T(8,128)(2,1)} %copy.102, f32[8,4,8,256,128,3]{4,3,5,2,1,0:T(8,128)} %get-tuple-element.41, f32[8,3,128]{2,1,0:T(4,128)S(1)} %add_divide_fusion, f32[8,3,128]{2,1,0:T(4,128)S(1)} %max.23, pred[4,8]{1,0:T(4,128)(4,1)S(1)} %iota_compare_fusion.1), kind=kOutput, calls=%fused_computation.20 | convolution fusion | flops 6568280064 | bytes 119037984 | tf_op jit(solution)/shard_map/grtoks,oksgd->tgrd/dot_general | solution.py:51
  1127.6 19.4 %fusion.8 = f32[128,8192]{1,0:T(8,128)} fusion(bf16[2,3072,8192]{2,1,0:T(8,128)(2,1)} %param.25, f32[128,3072]{1,0:T(8,128)S(1)} %get-tuple-element.45, f32[3072]{0:T(1024)S(1)} %bitcast.299, f32[128]{0:T(128)S(1)} %add_rsqrt_fusion), kind=kOutput, calls=%fused_computation.18 | convolution fusion | flops 6443630592 | bytes 56111616 | tf_op jit(solution)/shard_map/dot_general | solution.py:55
  1147.0 35.5 %fusion.109 = bf16[1,128,3072]{2,1,0:T(8,128)(2,1)} fusion(f32[128,3072]{1,0:T(8,128)S(1)} %get-tuple-element.45, bf16[2,8192,3072]{2,1,0:T(8,128)(2,1)} %param.27, bf16[2,3072,8192]{2,1,0:T(8,128)(2,1)} %param.26, f32[128,8192]{1,0:T(8,128)} %fusion.8, f32[3072]{0:T(1024)S(1)} %bitcast.300, f32[128]{0:T(128)S(1)} %add_rsqrt_fusion), kind=kOutput, calls=%fused_computation.85 | convolution fusion | flops 12893159424 | bytes 108802560 | tf_op jit(solution)/shard_map/dot_general | solution.py:58
  (99 shorter events, 130.4 us)
Async XLA Ops:
  129.8 373.2 %all-to-all-start = ((bf16[4,8,2,256,8,128]{5,3,1,4,2,0:T(8,128)(2,1)}), bf16[4,8,2,256,8,128]{5,3,1,4,2,0:T(8,128)(2,1)}, u32[]{:S(2)}, u32[]{:S(2)}) async-start(bf16[4,8,2,256,8,128]{5,3,1,4,2,0:T(8,128)(2,1)} %copy.54), calls=%async_computation | async-start | bytes 67108864 | tf_op jit(solution)/shard_map/all_to_all | solution.py:79
  208.2 23.2 %copy-start.1 = (bf16[1,128,3072]{2,1,0:T(8,128)(2,1)S(1)}, bf16[1,128,3072]{2,1,0:T(8,128)(2,1)}, u32[]{:S(2)}) copy-start(bf16[1,128,3072]{2,1,0:T(8,128)(2,1)} %param.18) | copy-start | bytes 2359300
  208.2 23.5 %copy-start.18 = (s32[1,4]{1,0:T(1,128)S(1)}, s32[1,4]{1,0:T(1,128)}, u32[]{:S(2)}) copy-start(s32[1,4]{1,0:T(1,128)} %param.17) | copy-start | bytes 52
  208.2 23.8 %copy-start.13 = (bf16[2,3072]{1,0:T(2,128)(2,1)S(1)}, bf16[2,3072]{1,0:T(2,128)(2,1)}, u32[]{:S(2)}) copy-start(bf16[2,3072]{1,0:T(2,128)(2,1)} %param.19) | copy-start | bytes 36868
  231.9 316.7 %copy-start.5 = (f32[128,64]{0,1:T(8,128)}, f32[128,64]{0,1:T(8,128)S(1)}, u32[]{:S(2)}) copy-start(f32[128,64]{0,1:T(8,128)S(1)} %get-tuple-element.30) | copy-start | bytes 98308
  232.0 316.7 %copy-start.7 = (f32[128,64]{0,1:T(8,128)}, f32[128,64]{0,1:T(8,128)S(1)}, u32[]{:S(2)}) copy-start(f32[128,64]{0,1:T(8,128)S(1)} %get-tuple-element.31) | copy-start | bytes 98308
  232.6 9.6 copy-start
  232.6 11.5 slice-start
  232.6 11.5 slice-start.1
  246.4 267.9 %copy-start.10 = (bf16[128,1024]{1,0:T(8,128)(2,1)S(1)}, bf16[128,1024]{1,0:T(8,128)(2,1)}, u32[]{:S(2)}) copy-start(bf16[128,1024]{1,0:T(8,128)(2,1)} %fusion.124) | copy-start | bytes 786436
  503.0 372.4 %all-to-all-start.1 = ((bf16[4,8,2,256,8,128]{5,3,1,4,2,0:T(8,128)(2,1)}), bf16[4,8,2,256,8,128]{5,3,1,4,2,0:T(8,128)(2,1)}, u32[]{:S(2)}, u32[]{:S(2)}) async-start(bf16[4,8,2,256,8,128]{5,3,1,4,2,0:T(8,128)(2,1)} %copy.65), calls=%async_computation.1 | async-start | bytes 67108864 | tf_op jit(solution)/shard_map/all_to_all | solution.py:79
  539.9 8.8 copy-start.11
  539.9 9.6 copy-start.14
  667.3 46.8 %copy-start.4 = (bf16[128,1024]{0,1:T(8,128)(2,1)S(1)}, bf16[128,1024]{0,1:T(8,128)(2,1)}, u32[]{:S(2)}) copy-start(bf16[128,1024]{0,1:T(8,128)(2,1)} %copy.95) | copy-start | bytes 786436
  667.3 48.7 %copy-start.2 = (bf16[1,128,3072]{2,1,0:T(8,128)(2,1)S(1)}, bf16[1,128,3072]{2,1,0:T(8,128)(2,1)}, u32[]{:S(2)}) copy-start(bf16[1,128,3072]{2,1,0:T(8,128)(2,1)} %param.18) | copy-start | bytes 2359300
  898.5 21.7 %copy-start.17 = (f32[1,3072]{1,0:T(1,128)S(1)}, f32[1,3072]{1,0:T(1,128)}, u32[]{:S(2)}) copy-start(f32[1,3072]{1,0:T(1,128)} %get-tuple-element.25) | copy-start | bytes 36868
  898.5 21.7 %copy-start.19 = (f32[128,3072]{1,0:T(8,128)S(1)}, f32[128,3072]{1,0:T(8,128)}, u32[]{:S(2)}) copy-start(f32[128,3072]{1,0:T(8,128)} %get-tuple-element.37) | copy-start | bytes 4718596
  939.7 39.2 %copy-start.15 = (f32[1,3072]{1,0:T(1,128)S(1)}, f32[1,3072]{1,0:T(1,128)}, u32[]{:S(2)}) copy-start(f32[1,3072]{1,0:T(1,128)} %get-tuple-element.26) | copy-start | bytes 36868
  978.9 5.0 copy-start.3
  983.9 9.1 copy-start.6
  983.9 9.1 copy-start.8
  998.7 41.2 %copy-start.12 = (pred[128,128]{0,1:T(8,128)(4,1)S(1)}, pred[128,128]{0,1:T(8,128)(4,1)}, u32[]{:S(2)}) copy-start(pred[128,128]{0,1:T(8,128)(4,1)} %iota_compare_fusion) | copy-start | bytes 49156
  1040.6 31.5 %copy-start.9 = (bf16[128,1024]{1,0:T(8,128)(2,1)S(1)}, bf16[128,1024]{1,0:T(8,128)(2,1)}, u32[]{:S(2)}) copy-start(bf16[128,1024]{1,0:T(8,128)(2,1)} %fusion.127) | copy-start | bytes 786436
  1118.1 9.5 copy-start.16
  (1 other events, 2.7 us)
where the time goes:
time: 1190 us; the launch traced here: 1180 us
  waiting for transfers between devices  406 us (34%)
  matrix products  343 us (29%)
  local copies, waits for them, and re-layouts  302 us (25%)
  other arithmetic  112 us (9%)
  starting transfers between devices  19.6 us (2%)
    all_to_all x2, waiting for transfers between devices, per_device(): incoming = lax.all_to_all(outgoing, 'pool', 0, 0, tiled=True)  406 us
    dot_general x2, matrix products, decoder_layer(): jnp.einsum('grtoks,oksgd->tgrd', prob_pre, v_pre, preferred_element_type=...  92.1 us
    dot_general x2, matrix products, decoder_layer(): jnp.einsum('tgrd,oksgd->grtoks', q_group, k_pre, preferred_element_type=j...  82.1 us
    dot_general x2, matrix products, decoder_layer(): jnp.dot(gated, wd_l, preferred_element_type=jnp.float32)  74.7 us
    dot_general x3, local copies, waits for them, and re-layouts, decoder_layer(): jnp.dot(h_attn, wq_l, preferred_element_type=jnp.float32)  74.2 us
    reduce_sum x2, other arithmetic, decoder_layer(): jnp.sum(exp_pre, axis=(3, 4, 5)) + jnp.sum(exp_new, axis=3)  62.4 us
    reshape x2, local copies, waits for them, and re-layouts, per_device(): jnp.take(pool_loc[layer], send_rows, axis=0)  46.3 us
    slice x2, local copies, waits for them, and re-layouts, decoder_layer(): v_pre = incoming[:, :, 1]  46.3 us
  transfers between devices with their start and end apart: 2, of which 2 were waited for; matrix products, arithmetic and copies ran while one was open for 27% of the time, Pallas kernels for 0%

commit v1 on v0

v1 whole, which is shorter than its diff:
```python
import functools

import jax
import jax.numpy as jnp
from jax import lax
from jax.experimental import pallas as pl
from jax.experimental.pallas import tpu as pltpu
from jax.sharding import PartitionSpec as P

EPS = 1e-5
ROPE_BASE = 500000.0
NEG = -1e30
LOG2E = 1.4426950408889634

TOKENS = 128
DM = 3072
HEAD = 128
QPK = 3
LANES = QPK * TOKENS
HALF_KV = 4
HALF_Q = HALF_KV * QPK * HEAD
PAGE = 256
PAGES = 16
SLOTS = 8
GROUP = 4
META = GROUP * SLOTS + GROUP
FF = 8192
FF_HALF = FF // 2
SCALE2 = HEAD ** -0.5 * LOG2E

MATE = [(0, 1), (1, 0), (2, 3), (3, 2)]
ACROSS = [(0, 2), (2, 0), (1, 3), (3, 1)]


def params(mb, sem=None):
    return pltpu.CompilerParams(vmem_limit_bytes=mb * 1024 * 1024, dimension_semantics=sem)


def f32dot(lhs, rhs):
    return jnp.dot(lhs, rhs, preferred_element_type=jnp.float32)


def normed(vals, gain):
    vals_f = vals.astype(jnp.float32)
    inv_rms = lax.rsqrt(jnp.mean(vals_f * vals_f, axis=-1, keepdims=True) + EPS)
    return (vals_f * inv_rms * gain.astype(jnp.float32)).astype(jnp.bfloat16)


def prep_body(me, page_ref, mine_ref, mate_ref, scr):
    core = me[0] % 2
    for kv in range(2):
        scr[kv] = page_ref[0, 0, kv].astype(jnp.float32).reshape(PAGE * 8, HEAD)
    for out_ref, half in ((mine_ref, core), (mate_ref, 1 - core)):
        for h in range(HALF_KV):
            rows = pl.ds(half * HALF_KV + h, PAGE, stride=8)
            out_ref[0, 0, h] = scr[0, rows, :].astype(jnp.bfloat16)
            val_t = scr[1, rows, :].T.astype(jnp.bfloat16)
            out_ref[0, 1, h, 0:128, :] = val_t[:, 0:128]
            out_ref[0, 1, h, 128:256, :] = val_t[:, 128:256]


def prep(me, pool, layer):
    shape = jax.ShapeDtypeStruct((PAGES, 2, HALF_KV, PAGE, HEAD), jnp.bfloat16)
    out_spec = pl.BlockSpec((1, 2, HALF_KV, PAGE, HEAD), lambda p, me: (p, 0, 0, 0, 0))
    return pl.pallas_call(
        prep_body,
        name="prep",
        out_shape=(shape, shape),
        grid_spec=pltpu.PrefetchScalarGridSpec(
            num_scalar_prefetch=1,
            grid=(PAGES,),
            in_specs=[pl.BlockSpec((1, 1, 2, PAGE, 8, HEAD), lambda p, me: (layer, p, 0, 0, 0, 0))],
            out_specs=[out_spec, out_spec],
            scratch_shapes=[pltpu.VMEM((2, PAGE * 8, HEAD), jnp.float32)],
        ),
        compiler_params=params(16, ("arbitrary",)),
        cost_estimate=pl.CostEstimate(flops=20_000_000_000, bytes_accessed=33_554_432, transcendentals=0),
    )(me, pool)


def rope_t(proj_t, cos_t, sin_t):
    first = proj_t[0:64]
    second = proj_t[64:128]
    return jnp.concatenate([first * cos_t - second * sin_t, second * cos_t + first * sin_t], axis=0)


def qkv_body(layer, with_kv, me, *refs):
    if with_kv:
        xa, xb, gain, cos_ref, sin_ref, wq, wk, wv, q_out, k_out, v_out, hx = refs
    else:
        xa, xb, gain, cos_ref, sin_ref, wq, q_out, hx = refs

    @pl.when(pl.program_id(0) == 0)
    def _():
        g = gain[layer:layer + 1, :]
        hx[0:TOKENS] = normed(xa[...], g)
        hx[TOKENS:2 * TOKENS] = normed(xb[...], g)

    cos_t = cos_ref[...]
    sin_t = sin_ref[...]
    hv = hx[...]
    q = f32dot(hv, wq[0])
    for r in range(2):
        for j in range(QPK):
            tile = q[r * TOKENS:(r + 1) * TOKENS, j * HEAD:(j + 1) * HEAD]
            q_out[r, 0, :, j * TOKENS:(j + 1) * TOKENS] = rope_t(tile.T, cos_t, sin_t).astype(jnp.bfloat16)
    if with_kv:
        k = f32dot(hv, wk[0])
        v = f32dot(hv, wv[0])
        for r in range(2):
            rows = slice(r * TOKENS, (r + 1) * TOKENS)
            k_out[r, 0] = rope_t(k[rows].T, cos_t, sin_t).T.astype(jnp.bfloat16)
            v_out[r, 0] = v[rows].T.astype(jnp.bfloat16)


def qkv(me, layer, xa, xb, gain, cos_t, sin_t, wq, wk=None, wv=None):
    with_kv = wk is not None
    whole = lambda shape: pl.BlockSpec(shape, lambda h, me: (0,) * len(shape))
    cols = lambda width: pl.BlockSpec((1, DM, width), lambda h, me: (layer, 0, (me[0] % 2) * HALF_KV + h))
    in_specs = [whole((TOKENS, DM)), whole((TOKENS, DM)), whole((2, DM)), whole((64, TOKENS)), whole((64, TOKENS)), cols(QPK * HEAD)]
    out_specs = [pl.BlockSpec((2, 1, HEAD, LANES), lambda h, me: (0, h, 0, 0))]
    out_shape = [jax.ShapeDtypeStruct((2, HALF_KV, HEAD, LANES), jnp.bfloat16)]
    args = [xa, xb, gain, cos_t, sin_t, wq]
    if with_kv:
        in_specs += [cols(HEAD), cols(HEAD)]
        out_specs += [pl.BlockSpec((2, 1, HEAD, HEAD), lambda h, me: (0, h, 0, 0))] * 2
        out_shape += [jax.ShapeDtypeStruct((2, HALF_KV, HEAD, HEAD), jnp.bfloat16)] * 2
        args += [wk, wv]
    flops = 2 * 2 * TOKENS * DM * (HALF_Q + (2 * HALF_KV * HEAD if with_kv else 0))
    return pl.pallas_call(
        functools.partial(qkv_body, layer, with_kv),
        name="qkv",
        out_shape=out_shape,
        grid_spec=pltpu.PrefetchScalarGridSpec(
            num_scalar_prefetch=1,
            grid=(HALF_KV,),
            in_specs=in_specs,
            out_specs=out_specs,
            scratch_shapes=[pltpu.VMEM((2 * TOKENS, DM), jnp.bfloat16)],
        ),
        compiler_params=params(32, ("arbitrary",)),
        cost_estimate=pl.CostEstimate(flops=flops, bytes_accessed=flops // 256, transcendentals=0),
    )(me, *args)


def attn_body(remote, me_ref, meta, *refs):
    if remote:
        q_ref, kv_own, kv_mate, o_ref, ml_ref, buf, acc, ml, sem = refs
    else:
        q_ref, k_new, v_new, kv_own, kv_mate, o_ref, ml_ref, buf, acc, ml, sem = refs
    me = me_ref[0]
    mate = me + 1 - 2 * (me % 2)

    def start(owner_is_me, page, slot):
        @pl.when(owner_is_me)
        def _():
            pltpu.make_async_copy(kv_own.at[page], buf.at[slot], sem.at[slot]).start()

        @pl.when(jnp.logical_not(owner_is_me))
        def _():
            pltpu.make_async_copy(kv_mate.at[page], buf.at[slot], sem.at[slot]).start()

    def request(r, carry):
        base = me if not remote else me + 2 - 4 * (me // 2)
        req = jnp.where(r == 0, base, base + 1 - 2 * (base % 2))
        n_own = meta[req * META + GROUP * SLOTS + me]
        n_all = n_own + meta[req * META + GROUP * SLOTS + mate]

        def fetch(t):
            is_own = t < n_own
            owner = jnp.where(is_own, me, mate)
            j = jnp.where(is_own, t, t - n_own)
            start(is_own, meta[owner * META + req * SLOTS + j], t % 2)

        @pl.when(n_all > 0)
        def _():
            fetch(0)

        for h in range(HALF_KV):
            if remote:
                acc[h] = jnp.zeros((HEAD, LANES), jnp.float32)
                ml[h, 0:1] = jnp.full((1, LANES), NEG, jnp.float32)
                ml[h, 1:2] = jnp.zeros((1, LANES), jnp.float32)
            else:
                s = f32dot(k_new[r, h], q_ref[r, h])
                key = lax.broadcasted_iota(jnp.int32, (TOKENS, LANES), 0)
                tok = lax.broadcasted_iota(jnp.int32, (TOKENS, LANES), 1) % TOKENS
                s = jnp.where(key <= tok, s, NEG)
                m = jnp.max(s, axis=0, keepdims=True)
                p = jnp.exp2((s - m) * SCALE2)
                ml[h, 0:1] = m
                ml[h, 1:2] = jnp.sum(p, axis=0, keepdims=True)
                acc[h] = f32dot(v_new[r, h], p.astype(jnp.bfloat16))

        def unit(t, c):
            slot = t % 2

            @pl.when(t + 1 < n_all)
            def _():
                fetch(t + 1)

            pltpu.make_async_copy(kv_own.at[0], buf.at[slot], sem.at[slot]).wait()
            for h in range(HALF_KV):
                s = f32dot(buf[slot, 0, h], q_ref[r, h])
                m_old = ml[h, 0:1]
                m = jnp.maximum(m_old, jnp.max(s, axis=0, keepdims=True))
                p = jnp.exp2((s - m) * SCALE2)
                keep = jnp.exp2((m_old - m) * SCALE2)
                ml[h, 0:1] = m
                ml[h, 1:2] = ml[h, 1:2] * keep + jnp.sum(p, axis=0, keepdims=True)
                val_t = jnp.concatenate([buf[slot, 1, h, 0:128, :], buf[slot, 1, h, 128:256, :]], axis=1)
                acc[h] = acc[h] * keep + f32dot(val_t, p.astype(jnp.bfloat16))
            return c

        lax.fori_loop(0, n_all, unit, 0)
        for h in range(HALF_KV):
            o_ref[r, h] = acc[h]
            ml_ref[r, h] = ml[h]
        return carry

    lax.fori_loop(0, 2, request, 0)


def attn(me, meta, q, kv_own, kv_mate, k_new=None, v_new=None):
    remote = k_new is None
    vmem = pl.BlockSpec(memory_space=pltpu.VMEM)
    hbm = pl.BlockSpec(memory_space=pltpu.HBM)
    args = [q] if remote else [q, k_new, v_new]
    return pl.pallas_call(
        functools.partial(attn_body, remote),
        name="attn",
        out_shape=(
            jax.ShapeDtypeStruct((2, HALF_KV, HEAD, LANES), jnp.float32),
            jax.ShapeDtypeStruct((2, HALF_KV, 8, LANES), jnp.float32),
        ),
        grid_spec=pltpu.PrefetchScalarGridSpec(
            num_scalar_prefetch=2,
            grid=(),
            in_specs=[vmem] * len(args) + [hbm, hbm],
            out_specs=[vmem, vmem],
            scratch_shapes=[
                pltpu.VMEM((2, 2, HALF_KV, PAGE, HEAD), jnp.bfloat16),
                pltpu.VMEM((HALF_KV, HEAD, LANES), jnp.float32),
                pltpu.VMEM((HALF_KV, 8, LANES), jnp.float32),
                pltpu.SemaphoreType.DMA((2,)),
            ],
        ),
        compiler_params=params(24),
        cost_estimate=pl.CostEstimate(flops=8_000_000_000, bytes_accessed=10_000_000, transcendentals=0),
    )(me, meta, *args, kv_own, kv_mate)


def merge_body(o1, ml1, o2, ml2, a_ref):
    m1, l1 = ml1[0, 0, 0:1], ml1[0, 0, 1:2]
    m2, l2 = ml2[0, 0, 0:1], ml2[0, 0, 1:2]
    m = jnp.maximum(m1, m2)
    w1 = jnp.exp2((m1 - m) * SCALE2)
    w2 = jnp.exp2((m2 - m) * SCALE2)
    inv = 1.0 / (l1 * w1 + l2 * w2)
    out = o1[0, 0] * (w1 * inv) + o2[0, 0] * (w2 * inv)
    for j in range(QPK):
        a_ref[0, :, j * HEAD:(j + 1) * HEAD] = out[:, j * TOKENS:(j + 1) * TOKENS].T.astype(jnp.bfloat16)


def merge(o1, ml1, o2, ml2):
    o_spec = pl.BlockSpec((1, 1, HEAD, LANES), lambda r, h: (r, h, 0, 0))
    ml_spec = pl.BlockSpec((1, 1, 8, LANES), lambda r, h: (r, h, 0, 0))
    return pl.pallas_call(
        merge_body,
        name="merge",
        out_shape=jax.ShapeDtypeStruct((2, TOKENS, HALF_Q), jnp.bfloat16),
        grid=(2, HALF_KV),
        in_specs=[o_spec, ml_spec, o_spec, ml_spec],
        out_specs=pl.BlockSpec((1, TOKENS, LANES), lambda r, h: (r, 0, h)),
        compiler_params=params(8),
    )(o1, ml1, o2, ml2)


WO_BLK = 512


def wo_body(layer, me, a_own, a_mate, xa, xb, gain, wo, x1_ref, h2_ref, scr):
    core = me[0] % 2
    n = pl.program_id(0)

    @pl.when(n == 0)
    def _():
        own = pl.ds(pl.multiple_of(core * HALF_Q, HALF_Q), HALF_Q)
        other = pl.ds(pl.multiple_of((1 - core) * HALF_Q, HALF_Q), HALF_Q)
        scr[0:TOKENS, own] = a_own[0]
        scr[TOKENS:2 * TOKENS, own] = a_own[1]
        scr[0:TOKENS, other] = a_mate[1]
        scr[TOKENS:2 * TOKENS, other] = a_mate[0]

    prod = f32dot(scr[...], wo[0])
    cols = pl.ds(pl.multiple_of(n * WO_BLK, WO_BLK), WO_BLK)
    x1_ref[0:TOKENS, cols] = (xa[...].astype(jnp.float32) + prod[0:TOKENS]).astype(jnp.bfloat16)
    x1_ref[TOKENS:2 * TOKENS, cols] = (xb[...].astype(jnp.float32) + prod[TOKENS:]).astype(jnp.bfloat16)

    @pl.when(n == pl.num_programs(0) - 1)
    def _():
        h2_ref[...] = normed(x1_ref[...], gain[layer:layer + 1, :])


def out_proj(me, layer, a_own, a_mate, xa, xb, gain, wo):
    whole = lambda shape: pl.BlockSpec(shape, lambda n, me: (0,) * len(shape))
    x_spec = pl.BlockSpec((TOKENS, WO_BLK), lambda n, me: (0, n))
    shape = jax.ShapeDtypeStruct((2 * TOKENS, DM), jnp.bfloat16)
    return pl.pallas_call(
        functools.partial(wo_body, layer),
        name="out_proj",
        out_shape=(shape, shape),
        grid_spec=pltpu.PrefetchScalarGridSpec(
            num_scalar_prefetch=1,
            grid=(DM // WO_BLK,),
            in_specs=[
                whole((2, TOKENS, HALF_Q)), whole((2, TOKENS, HALF_Q)), x_spec, x_spec, whole((2, DM)),
                pl.BlockSpec((1, DM, WO_BLK), lambda n, me: (layer, 0, n)),
            ],
            out_specs=[whole((2 * TOKENS, DM)), whole((2 * TOKENS, DM))],
            scratch_shapes=[pltpu.VMEM((2 * TOKENS, DM), jnp.bfloat16)],
        ),
        compiler_params=params(32, ("arbitrary",)),
        cost_estimate=pl.CostEstimate(flops=4_800_000_000, bytes_accessed=20_000_000, transcendentals=0),
    )(me, a_own, a_mate, xa, xb, gain, wo)


FF_BLK = 256


def mlp_body(me, h2, wg, wu, wd, y_own, y_mate):
    hv = h2[...]
    gate = f32dot(hv, wg[0])
    up = f32dot(hv, wu[0])
    gated = (jax.nn.silu(gate) * up).astype(jnp.bfloat16)
    y = f32dot(gated, wd[0])

    @pl.when(pl.program_id(0) == 0)
    def _():
        y_own[...] = y[0:TOKENS]
        y_mate[...] = y[TOKENS:]

    @pl.when(pl.program_id(0) > 0)
    def _():
        y_own[...] += y[0:TOKENS]
        y_mate[...] += y[TOKENS:]


def mlp(me, layer, h2, wg, wu, wd):
    blocks = FF_HALF // FF_BLK
    whole = lambda shape: pl.BlockSpec(shape, lambda n, me: (0,) * len(shape))
    cols = pl.BlockSpec((1, DM, FF_BLK), lambda n, me: (layer, 0, (me[0] % 2) * blocks + n))
    rows = pl.BlockSpec((1, FF_BLK, DM), lambda n, me: (layer, (me[0] % 2) * blocks + n, 0))
    shape = jax.ShapeDtypeStruct((TOKENS, DM), jnp.float32)
    return pl.pallas_call(
        mlp_body,
        name="mlp",
        out_shape=(shape, shape),
        grid_spec=pltpu.PrefetchScalarGridSpec(
            num_scalar_prefetch=1,
            grid=(blocks,),
            in_specs=[whole((2 * TOKENS, DM)), cols, cols, rows],
            out_specs=[whole((TOKENS, DM)), whole((TOKENS, DM))],
        ),
        compiler_params=params(40, ("arbitrary",)),
        cost_estimate=pl.CostEstimate(flops=19_000_000_000, bytes_accessed=76_000_000, transcendentals=0),
    )(me, h2, wg, wu, wd)


def solution(mesh):
    by_request = P(('replica', 'pool'))
    by_owner = P(None, ('replica', 'pool'))
    shared = P()

    def per_device(pool_loc, idx_loc, count_loc, x_loc, norm_attn, wq, wk, wv, wo, norm_mlp, w_gate, w_up, w_down):
        layers = pool_loc.shape[0]
        to_mate = lambda arr: lax.ppermute(arr, 'pool', MATE)
        to_across = lambda arr: lax.ppermute(arr, 'pool', ACROSS)
        me = lax.axis_index('pool').astype(jnp.int32).reshape(1)
        meta = lax.all_gather(jnp.concatenate([idx_loc.reshape(-1), count_loc.reshape(-1)]), 'pool', tiled=True)
        half = HEAD // 2
        freqs = ROPE_BASE ** (-jnp.arange(half, dtype=jnp.float32) / half)
        angles = freqs[:, None] * jnp.arange(TOKENS, dtype=jnp.float32)[None, :]
        cos_t = jnp.cos(angles)
        sin_t = jnp.sin(angles)
        pages = []
        for layer in range(layers):
            mine, theirs = prep(me, pool_loc, layer)
            pages.append((mine, to_mate(theirs)))
        x = x_loc[0]
        for layer in range(layers):
            kv_own, kv_mate = pages[layer]
            x_mate = to_mate(x)
            x_across = to_across(x)
            x_diag = to_mate(x_across)
            q_loc, k_new, v_new = qkv(me, layer, x, x_mate, norm_attn, cos_t, sin_t, wq, wk, wv)
            q_rem, = qkv(me, layer, x_across, x_diag, norm_attn, cos_t, sin_t, wq)
            o_send, ml_send = attn(me, meta, q_rem, kv_own, kv_mate)
            o_rem = to_across(o_send)
            ml_rem = to_across(ml_send)
            o_loc, ml_loc = attn(me, meta, q_loc, kv_own, kv_mate, k_new, v_new)
            a_own = merge(o_loc, ml_loc, o_rem, ml_rem)
            a_mate = to_mate(a_own)
            x1, h2 = out_proj(me, layer, a_own, a_mate, x, x_mate, norm_mlp, wo)
            y_own, y_send = mlp(me, layer, h2, w_gate, w_up, w_down)
            y_got = to_mate(y_send)
            x = (x1[:TOKENS].astype(jnp.float32) + (y_own + y_got)).astype(jnp.bfloat16)
        return x[None]

    return jax.shard_map(per_device, mesh=mesh, in_specs=(by_owner, by_owner, by_request, by_request, shared, shared, shared, shared, shared, shared, shared, shared, shared), out_specs=by_request, check_vma=False)
```

time: 1190 us -> 370 us (0.31)
  waiting for transfers between devices: 406 us -> 49.7 us
  matrix products: 343 us -> 0 us
  local copies, waits for them, and re-layouts: 302 us -> 18 us
  Pallas kernels: 0 us -> 281 us
  other arithmetic: 112 us -> 2.52 us
    all_to_all x2 -> x0, waiting for transfers between devices: 406 us -> none  [per_device(): incoming = lax.all_to_all(outgoing, 'pool', 0, 0, tiled=True)]
    dot_general x20 -> x0, matrix products: 343 us -> none  [the longest x2 92.1 us: decoder_layer(): jnp.einsum('grtoks,oksgd->tgrd', prob_pre, v_pre, preferred_element_type=...]
    pallas_call x0 -> x16, Pallas kernels: none -> 281 us  [the longest x4 108 us: attn(): pl.pallas_call(functools.partial(attn_body, remote), name='attn', out_sha...]
    dot_general x6 -> x0, local copies, waits for them, and re-layouts: 102 us -> none  [the longest x3 74.2 us: decoder_layer(): jnp.dot(h_attn, wq_l, preferred_element_type=jnp.float32)]
    reduce_sum x5 -> x0, other arithmetic: 63.2 us -> none  [the longest x2 62.4 us: decoder_layer(): jnp.sum(exp_pre, axis=(3, 4, 5)) + jnp.sum(exp_new, axis=3)]
    ppermute x0 -> x16, waiting for transfers between devices: none -> 49.7 us  [the longest x6 38 us: per_device(): to_across = lambda arr: lax.ppermute(arr, 'pool', ACROSS)]
    reshape x5 -> x1, local copies, waits for them, and re-layouts: 47.4 us -> 0.09 us  [per_device(): idx_loc.reshape(-1)]
    slice x2 -> x0, local copies, waits for them, and re-layouts: 46.3 us -> none  [decoder_layer(): v_pre = incoming[:, :, 1]]
  transfers between devices with their start and end apart: 2 -> 16, of which waited for: 2 -> 7; matrix products, arithmetic and copies ran while one was open for 27% -> 1% of each run, Pallas kernels for 0% -> 58%
where the time goes in v1:
time: 370 us; the launch traced here: 366 us
  Pallas kernels  281 us (76%)
  waiting for transfers between devices  49.7 us (13%)
  local copies, waits for them, and re-layouts  18 us (5%)
  starting transfers between devices  9.36 us (3%)
  blocking collectives  5.15 us (1%)
    pallas_call x4, Pallas kernels, attn(): pl.pallas_call(functools.partial(attn_body, remote), name='attn', out_sha...  108 us
    pallas_call x2, Pallas kernels, mlp(): pl.pallas_call(mlp_body, name='mlp', out_shape=(shape, shape), grid_spec=...  73 us
    ppermute x6, waiting for transfers between devices, per_device(): to_across = lambda arr: lax.ppermute(arr, 'pool', ACROSS)  38 us
    pallas_call x2, Pallas kernels, prep(): pl.pallas_call(prep_body, name='prep', out_shape=(shape, shape), grid_spe...  37.6 us
    pallas_call x4, Pallas kernels, qkv(): pl.pallas_call(functools.partial(qkv_body, layer, with_kv), name='qkv', o...  37.5 us
    pallas_call x2, Pallas kernels, out_proj(): pl.pallas_call(functools.partial(wo_body, layer), name='out_proj', out_sh...  22.2 us
    unnamed x33, local copies, waits for them, and re-layouts  17.9 us
    ppermute x10, waiting for transfers between devices, per_device(): to_mate = lambda arr: lax.ppermute(arr, 'pool', MATE)  11.7 us
  transfers between devices with their start and end apart: 16, of which 7 were waited for; matrix products, arithmetic and copies ran while one was open for 1% of the time, Pallas kernels for 58%

profile of v1, /device:TPU:0, one launch (start us, length us, event | category | flops | bytes accessed | tf_op | source)
XLA Modules:
  0.0 366.4 jit_solution(6102087716520903825)
XLA Ops:
  0.0 18.1 %prep.2 = (bf16[16,2,4,256,128]{4,3,2,1,0:T(8,128)(2,1)S(1)}, bf16[16,2,4,256,128]{4,3,2,1,0:T(8,128)(2,1)}) custom-call(s32[1]{0:T(128)} %bitcast.me.me_ref, bf16[2,16,2,256,8,128]{5,4,3,2,1,0:T(8,128)(2,1)} %page_ref.3), custom_call_target="tpu_custom_call" | custom-call | flops 20000000000 | bytes 33554432 | tf_op jit(solution)/shard_map/prep/pallas_call | solution.py:65
  18.2 3.3 copy-done.6
  24.7 18.2 %collective-permute-done.2.refs_0_ = bf16[128,3072]{1,0:T(8,128)(2,1)S(1)} collective-permute-done((bf16[128,3072]{1,0:T(8,128)(2,1)S(1)}, bf16[128,3072]{1,0:T(8,128)(2,1)S(1)}, u32[]{:S(2)}, u32[]{:S(2)}) %collective-permute-start.2) | collective-permute-done | bytes 786464 | tf_op jit(solution)/shard_map/ppermute | solution.py:378
  46.2 5.2 %all-reduce.meta = s32[144]{0:T(256)S(1)} all-reduce(s32[144]{0:T(256)S(1)} %add_dynamic-update-slice_fusion), channel_id=1, replica_groups=mesh['replica'=4,'pool'=4] {'pool'}, use_global_device_ids=true, to_apply=%add | all-reduce | flops 144 | bytes 1152
  51.6 7.9 %qkv.5.refs_0_ = bf16[2,4,128,384]{3,2,1,0:T(8,128)(2,1)S(1)} custom-call(s32[1]{0:T(128)} %bitcast.me.me_ref, bf16[128,3072]{1,0:T(8,128)(2,1)S(1)} %collective-permute-done.2.refs_0_, bf16[128,3072]{1,0:T(8,128)(2,1)S(1)} %collective-permute-done.3.refs_1_, bf16[2,3072]{1,0:T(2,128)(2,1)S(1)} %copy-done.1, f32[64,128]{1,0:T(8,128)S(1)} %get-tuple-element.58.refs_3_, ...), custom_call_target="tpu_custom_call" | custom-call | flops 2415919104 | bytes 9437184 | tf_op jit(solution)/shard_map/qkv/pallas_call | solution.py:130
  59.5 27.5 %attn.5 = (f32[2,4,128,384]{3,2,1,0:T(8,128)S(1)}, f32[2,4,8,384]{3,2,1,0:T(8,128)S(1)}) custom-call(s32[1]{0:T(128)} %bitcast.me.me_ref, s32[144]{0:T(256)S(1)} %all-reduce.meta, bf16[2,4,128,384]{3,2,1,0:T(8,128)(2,1)S(1)} %qkv.5.refs_0_, bf16[16,2,4,256,128]{4,3,2,1,0:T(8,128)(2,1)S(1)} %copy-done.7, ...), custom_call_target="tpu_custom_call" | custom-call | flops 8000000000 | bytes 10000000 | tf_op jit(solution)/shard_map/attn/pallas_call | solution.py:229
  87.1 19.4 %prep.3 = (bf16[16,2,4,256,128]{4,3,2,1,0:T(8,128)(2,1)S(1)}, bf16[16,2,4,256,128]{4,3,2,1,0:T(8,128)(2,1)}) custom-call(s32[1]{0:T(128)} %bitcast.me.me_ref, bf16[2,16,2,256,8,128]{5,4,3,2,1,0:T(8,128)(2,1)} %page_ref.3), custom_call_target="tpu_custom_call" | custom-call | flops 20000000000 | bytes 33554432 | tf_op jit(solution)/shard_map/prep/pallas_call | solution.py:65
  106.5 3.2 copy-done.3
  109.8 11.0 %qkv.4 = (bf16[2,4,128,384]{3,2,1,0:T(8,128)(2,1)S(1)}, bf16[2,4,128,128]{3,2,1,0:T(8,128)(2,1)S(1)}, bf16[2,4,128,128]{3,2,1,0:T(8,128)(2,1)S(1)}) custom-call(s32[1]{0:T(128)} %bitcast.me.me_ref, bf16[128,3072]{1,0:T(8,128)(2,1)S(1)} %bitcast.10, bf16[128,3072]{1,0:T(8,128)(2,1)S(1)} %collective-permute-done.refs_1_.xb, bf16[2,3072]{1,0:T(2,128)(2,1)S(1)} %copy-done.1, ...), custom_call_target="tpu_custom_call" | custom-call | flops 4026531840 | bytes 15728640 | tf_op jit(solution)/shard_map/qkv/pallas_call | solution.py:130
  121.5 3.4 copy-done.8
  124.8 26.4 %attn.4 = (f32[2,4,128,384]{3,2,1,0:T(8,128)S(1)}, f32[2,4,8,384]{3,2,1,0:T(8,128)S(1)}) custom-call(s32[1]{0:T(128)} %bitcast.me.me_ref, s32[144]{0:T(256)S(1)} %all-reduce.meta, bf16[2,4,128,384]{3,2,1,0:T(8,128)(2,1)S(1)} %get-tuple-element.31.refs_0_, bf16[2,4,128,128]{3,2,1,0:T(8,128)(2,1)S(1)} %get-tuple-element.32.refs_1_, ...), custom_call_target="tpu_custom_call" | custom-call | flops 8000000000 | bytes 10000000 | tf_op jit(solution)/shard_map/attn/pallas_call | solution.py:229
  155.3 11.1 %out_proj.2 = (bf16[256,3072]{1,0:T(8,128)(2,1)S(1)}, bf16[256,3072]{1,0:T(8,128)(2,1)S(1)}) custom-call(s32[1]{0:T(128)} %bitcast.me.me_ref, bf16[2,128,1536]{2,1,0:T(8,128)(2,1)S(1)} %merge.2.a_own, bf16[2,128,1536]{2,1,0:T(8,128)(2,1)S(1)} %collective-permute-done.6.a_mate, bf16[128,3072]{1,0:T(8,128)(2,1)S(1)} %bitcast.11, ...), custom_call_target="tpu_custom_call" | custom-call | flops 4800000000 | bytes 20000000 | tf_op jit(solution)/shard_map/out_proj/pallas_call | solution.py:309
  166.4 36.6 %mlp.2 = (f32[128,3072]{1,0:T(8,128)S(1)}, f32[128,3072]{1,0:T(8,128)S(1)}) custom-call(s32[1]{0:T(128)} %bitcast.me.me_ref, bf16[256,3072]{1,0:T(8,128)(2,1)S(1)} %get-tuple-element.41.h2, bf16[2,3072,8192]{2,1,0:T(8,128)(2,1)} %wg.3, bf16[2,3072,8192]{2,1,0:T(8,128)(2,1)} %wu.3, bf16[2,8192,3072]{2,1,0:T(8,128)(2,1)} %wd.3), custom_call_target="tpu_custom_call" | custom-call | flops 19000000512 | bytes 76000000 | tf_op jit(solution)/shard_map/mlp/pallas_call | solution.py:355
  203.4 3.0 collective-permute-done.7
  206.7 19.8 %collective-permute-done.10.refs_0_ = bf16[128,3072]{1,0:T(8,128)(2,1)S(1)} collective-permute-done((bf16[128,3072]{1,0:T(8,128)(2,1)S(1)}, bf16[128,3072]{1,0:T(8,128)(2,1)S(1)}, u32[]{:S(2)}, u32[]{:S(2)}) %collective-permute-start.10) | collective-permute-done | bytes 786464 | tf_op jit(solution)/shard_map/ppermute | solution.py:378
  228.8 7.7 %qkv.7.refs_0_ = bf16[2,4,128,384]{3,2,1,0:T(8,128)(2,1)S(1)} custom-call(s32[1]{0:T(128)} %bitcast.me.me_ref, bf16[128,3072]{1,0:T(8,128)(2,1)S(1)} %collective-permute-done.10.refs_0_, bf16[128,3072]{1,0:T(8,128)(2,1)S(1)} %collective-permute-done.11.refs_1_, bf16[2,3072]{1,0:T(2,128)(2,1)S(1)} %copy-done.1, f32[64,128]{1,0:T(8,128)S(1)} %get-tuple-element.58.refs_3_, ...), custom_call_target="tpu_custom_call" | custom-call | flops 2415919104 | bytes 9437184 | tf_op jit(solution)/shard_map/qkv/pallas_call | solution.py:130
  236.5 3.4 copy-done.4
  239.9 27.5 %attn.7 = (f32[2,4,128,384]{3,2,1,0:T(8,128)S(1)}, f32[2,4,8,384]{3,2,1,0:T(8,128)S(1)}) custom-call(s32[1]{0:T(128)} %bitcast.me.me_ref, s32[144]{0:T(256)S(1)} %all-reduce.meta, bf16[2,4,128,384]{3,2,1,0:T(8,128)(2,1)S(1)} %qkv.7.refs_0_, bf16[16,2,4,256,128]{4,3,2,1,0:T(8,128)(2,1)S(1)} %copy-done.4, ...), custom_call_target="tpu_custom_call" | custom-call | flops 8000000000 | bytes 10000000 | tf_op jit(solution)/shard_map/attn/pallas_call | solution.py:229
  267.4 11.0 %qkv.6 = (bf16[2,4,128,384]{3,2,1,0:T(8,128)(2,1)S(1)}, bf16[2,4,128,128]{3,2,1,0:T(8,128)(2,1)S(1)}, bf16[2,4,128,128]{3,2,1,0:T(8,128)(2,1)S(1)}) custom-call(s32[1]{0:T(128)} %bitcast.me.me_ref, bf16[128,3072]{1,0:T(8,128)(2,1)S(1)} %add_convert_fusion.1.refs_0_.xa, bf16[128,3072]{1,0:T(8,128)(2,1)S(1)} %collective-permute-done.8.refs_1_.xb, ...), custom_call_target="tpu_custom_call" | custom-call | flops 4026531840 | bytes 15728640 | tf_op jit(solution)/shard_map/qkv/pallas_call | solution.py:130
  280.4 3.4 copy-done.5
  283.8 26.6 %attn.6 = (f32[2,4,128,384]{3,2,1,0:T(8,128)S(1)}, f32[2,4,8,384]{3,2,1,0:T(8,128)S(1)}) custom-call(s32[1]{0:T(128)} %bitcast.me.me_ref, s32[144]{0:T(256)S(1)} %all-reduce.meta, bf16[2,4,128,384]{3,2,1,0:T(8,128)(2,1)S(1)} %get-tuple-element.44.refs_0_, bf16[2,4,128,128]{3,2,1,0:T(8,128)(2,1)S(1)} %get-tuple-element.45.refs_1_, ...), custom_call_target="tpu_custom_call" | custom-call | flops 8000000000 | bytes 10000000 | tf_op jit(solution)/shard_map/attn/pallas_call | solution.py:229
  314.3 11.1 %out_proj.3 = (bf16[256,3072]{1,0:T(8,128)(2,1)S(1)}, bf16[256,3072]{1,0:T(8,128)(2,1)S(1)}) custom-call(s32[1]{0:T(128)} %bitcast.me.me_ref, bf16[2,128,1536]{2,1,0:T(8,128)(2,1)S(1)} %merge.3.a_own, bf16[2,128,1536]{2,1,0:T(8,128)(2,1)S(1)} %collective-permute-done.14.a_mate, bf16[128,3072]{1,0:T(8,128)(2,1)S(1)} %add_convert_fusion.1.refs_0_.xa, ...), custom_call_target="tpu_custom_call" | custom-call | flops 4800000000 | bytes 20000000 | tf_op jit(solution)/shard_map/out_proj/pallas_call | solution.py:309
  325.3 36.4 %mlp.3 = (f32[128,3072]{1,0:T(8,128)S(1)}, f32[128,3072]{1,0:T(8,128)S(1)}) custom-call(s32[1]{0:T(128)} %bitcast.me.me_ref, bf16[256,3072]{1,0:T(8,128)(2,1)S(1)} %get-tuple-element.54.h2, bf16[2,3072,8192]{2,1,0:T(8,128)(2,1)} %wg.3, bf16[2,3072,8192]{2,1,0:T(8,128)(2,1)} %wu.3, bf16[2,8192,3072]{2,1,0:T(8,128)(2,1)} %wd.3), custom_call_target="tpu_custom_call" | custom-call | flops 19000000512 | bytes 76000000 | tf_op jit(solution)/shard_map/mlp/pallas_call | solution.py:355
  362.2 3.0 collective-permute-done.15
  (66 shorter events, 21.4 us)
Async XLA Ops:
  0.0 22.2 %copy-start = (bf16[1,128,3072]{2,1,0:T(8,128)(2,1)S(1)}, bf16[1,128,3072]{2,1,0:T(8,128)(2,1)}, u32[]{:S(2)}) copy-start(bf16[1,128,3072]{2,1,0:T(8,128)(2,1)} %param.16) | copy-start | bytes 2359300
  0.0 44.0 %copy-start.9 = (s32[4,1,8]{2,1,0:T(1,128)S(1)}, s32[4,1,8]{2,1,0:T(1,128)}, u32[]{:S(2)}) copy-start(s32[4,1,8]{2,1,0:T(1,128)} %param.14) | copy-start | bytes 388
  0.0 44.7 %copy-start.11 = (u32[16]{0:T(128)S(1)}, u32[16]{0:T(128)}, u32[]{:S(2)}) copy-start(u32[16]{0:T(128)} %constant.14) | copy-start | bytes 196
  0.0 46.0 %copy-start.10 = (s32[1,4]{1,0:T(1,128)S(1)}, s32[1,4]{1,0:T(1,128)}, u32[]{:S(2)}) copy-start(s32[1,4]{1,0:T(1,128)} %param.15) | copy-start | bytes 52
  0.0 51.6 %copy-start.1 = (bf16[2,3072]{1,0:T(2,128)(2,1)S(1)}, bf16[2,3072]{1,0:T(2,128)(2,1)}, u32[]{:S(2)}) copy-start(bf16[2,3072]{1,0:T(2,128)(2,1)} %refs_2_.7) | copy-start | bytes 36868
  21.4 38.1 %collective-permute-start.1 = (bf16[16,2,4,256,128]{4,3,2,1,0:T(8,128)(2,1)}, bf16[16,2,4,256,128]{4,3,2,1,0:T(8,128)(2,1)}, u32[]{:S(2)}, u32[]{:S(2)}) collective-permute-start(bf16[16,2,4,256,128]{4,3,2,1,0:T(8,128)(2,1)} %get-tuple-element.35), channel_id=1, source_target_pairs={{0,1},{1,0},{2,3},{3,2},{4,5},{5,4},{6,7},{7,6},{8,9},{9,8},{10,11... | collective-permute-start | bytes 25165832 | tf_op jit(solution)/shard_map/ppermute | solution.py:377
  22.2 20.7 %collective-permute-start.2 = (bf16[128,3072]{1,0:T(8,128)(2,1)S(1)}, bf16[128,3072]{1,0:T(8,128)(2,1)S(1)}, u32[]{:S(2)}, u32[]{:S(2)}) collective-permute-start(bf16[128,3072]{1,0:T(8,128)(2,1)S(1)} %bitcast.8), channel_id=1, source_target_pairs={{0,2},{2,0},{1,3},{3,1},{4,6},{6,4},{5,7},{7,5},{8,10},{10,8},{9,1... | collective-permute-start | bytes 2359304 | tf_op jit(solution)/shard_map/ppermute | solution.py:378
  42.9 8.7 %collective-permute-start.3 = (bf16[128,3072]{1,0:T(8,128)(2,1)S(1)}, bf16[128,3072]{1,0:T(8,128)(2,1)S(1)}, u32[]{:S(2)}, u32[]{:S(2)}) collective-permute-start(bf16[128,3072]{1,0:T(8,128)(2,1)S(1)} %collective-permute-done.2.refs_0_), channel_id=1, source_target_pairs={{0,1},{1,0},{2,3},{3,2},{4,5},{5,4},{6,7},{7,6},{8,9},{9,8},{10,11... | collective-permute-start | bytes 2359304 | tf_op jit(solution)/shard_map/ppermute | solution.py:377
  42.9 66.8 %collective-permute-start = (bf16[128,3072]{1,0:T(8,128)(2,1)S(1)}, bf16[128,3072]{1,0:T(8,128)(2,1)S(1)}, u32[]{:S(2)}, u32[]{:S(2)}) collective-permute-start(bf16[128,3072]{1,0:T(8,128)(2,1)S(1)} %bitcast.9), channel_id=1, source_target_pairs={{0,1},{1,0},{2,3},{3,2},{4,5},{5,4},{6,7},{7,6},{8,9},{9,8},{10,11... | collective-permute-start | bytes 2359304 | tf_op jit(solution)/shard_map/ppermute | solution.py:377
  87.0 22.8 %slice-start = ((s8[12582912]{0:T(1024)(128)(4,1)}), s8[4194304]{0:T(1024)(128)(4,1)S(1)}, s32[]{:S(2)}) async-start(s8[12582912]{0:T(1024)(128)(4,1)} %bitcast.6), calls=%async_computation | async-start | bytes 8388608
  87.0 22.8 %slice-start.1 = ((s8[12582912]{0:T(1024)(128)(4,1)}), s8[4194304]{0:T(1024)(128)(4,1)S(1)}, s32[]{:S(2)}) async-start(s8[12582912]{0:T(1024)(128)(4,1)} %bitcast.6), calls=%async_computation.1 | async-start | bytes 8388608
  87.0 22.8 %slice-start.2 = ((s8[12582912]{0:T(1024)(128)(4,1)}), s8[4194304]{0:T(1024)(128)(4,1)S(1)}, s32[]{:S(2)}) async-start(s8[12582912]{0:T(1024)(128)(4,1)} %bitcast.6), calls=%async_computation.2 | async-start | bytes 8388608
  87.0 64.2 %collective-permute-start.4 = (f32[2,4,128,384]{3,2,1,0:T(8,128)S(1)}, f32[2,4,128,384]{3,2,1,0:T(8,128)S(1)}, u32[]{:S(2)}, u32[]{:S(2)}) collective-permute-start(f32[2,4,128,384]{3,2,1,0:T(8,128)S(1)} %get-tuple-element.38), channel_id=1, source_target_pairs={{0,2},{2,0},{1,3},{3,1},{4,6},{6,4},{5,7},{7,5},{8,10},{10,8},{9,1... | collective-permute-start | bytes 4718600 | tf_op jit(solution)/shard_map/ppermute | solution.py:378
  109.7 126.8 %collective-permute-start.9 = (bf16[16,2,4,256,128]{4,3,2,1,0:T(8,128)(2,1)}, bf16[16,2,4,256,128]{4,3,2,1,0:T(8,128)(2,1)}, u32[]{:S(2)}, u32[]{:S(2)}) collective-permute-start(bf16[16,2,4,256,128]{4,3,2,1,0:T(8,128)(2,1)} %get-tuple-element.48), channel_id=1, source_target_pairs={{0,1},{1,0},{2,3},{3,2},{4,5},{5,4},{6,7},{7,6},{8,9},{9,8},{10,11... | collective-permute-start | bytes 25165832 | tf_op jit(solution)/shard_map/ppermute | solution.py:377
  120.8 30.4 %collective-permute-start.5 = (f32[2,4,8,384]{3,2,1,0:T(8,128)S(1)}, f32[2,4,8,384]{3,2,1,0:T(8,128)S(1)}, u32[]{:S(2)}, u32[]{:S(2)}) collective-permute-start(f32[2,4,8,384]{3,2,1,0:T(8,128)S(1)} %get-tuple-element.39), channel_id=1, source_target_pairs={{0,2},{2,0},{1,3},{3,1},{4,6},{6,4},{5,7},{7,5},{8,10},{10,8},{9,1... | collective-permute-start | bytes 294920 | tf_op jit(solution)/shard_map/ppermute | solution.py:378
  152.5 2.8 collective-permute-start.6
  203.0 3.4 collective-permute-start.7
  206.7 19.8 %collective-permute-start.10 = (bf16[128,3072]{1,0:T(8,128)(2,1)S(1)}, bf16[128,3072]{1,0:T(8,128)(2,1)S(1)}, u32[]{:S(2)}, u32[]{:S(2)}) collective-permute-start(bf16[128,3072]{1,0:T(8,128)(2,1)S(1)} %add_convert_fusion.1.refs_0_.xa), channel_id=1, source_target_pairs={{0,2},{2,0},{1,3},{3,1},{4,6},{6,4},{5,7},{7,5},{8,10},{10,8},{9,1... | collective-permute-start | bytes 2359304 | tf_op jit(solution)/shard_map/ppermute | solution.py:378
  226.5 2.3 collective-permute-start.11
  226.5 40.9 %collective-permute-start.8 = (bf16[128,3072]{1,0:T(8,128)(2,1)S(1)}, bf16[128,3072]{1,0:T(8,128)(2,1)S(1)}, u32[]{:S(2)}, u32[]{:S(2)}) collective-permute-start(bf16[128,3072]{1,0:T(8,128)(2,1)S(1)} %add_convert_fusion.1.refs_0_.xa), channel_id=1, source_target_pairs={{0,1},{1,0},{2,3},{3,2},{4,5},{5,4},{6,7},{7,6},{8,9},{9,8},{10,11... | collective-permute-start | bytes 2359304 | tf_op jit(solution)/shard_map/ppermute | solution.py:377
  267.4 43.0 %collective-permute-start.12 = (f32[2,4,128,384]{3,2,1,0:T(8,128)S(1)}, f32[2,4,128,384]{3,2,1,0:T(8,128)S(1)}, u32[]{:S(2)}, u32[]{:S(2)}) collective-permute-start(f32[2,4,128,384]{3,2,1,0:T(8,128)S(1)} %get-tuple-element.51), channel_id=1, source_target_pairs={{0,2},{2,0},{1,3},{3,1},{4,6},{6,4},{5,7},{7,5},{8,10},{10,8},{9,1... | collective-permute-start | bytes 4718600 | tf_op jit(solution)/shard_map/ppermute | solution.py:378
  278.4 32.0 %collective-permute-start.13 = (f32[2,4,8,384]{3,2,1,0:T(8,128)S(1)}, f32[2,4,8,384]{3,2,1,0:T(8,128)S(1)}, u32[]{:S(2)}, u32[]{:S(2)}) collective-permute-start(f32[2,4,8,384]{3,2,1,0:T(8,128)S(1)} %get-tuple-element.52), channel_id=1, source_target_pairs={{0,2},{2,0},{1,3},{3,1},{4,6},{6,4},{5,7},{7,5},{8,10},{10,8},{9,1... | collective-permute-start | bytes 294920 | tf_op jit(solution)/shard_map/ppermute | solution.py:378
  311.7 2.6 collective-permute-start.14
  361.7 3.4 collective-permute-start.15
  (7 other events, 28.6 us)

commit v2 on v1

v2 whole, which is shorter than its diff:
```python
import functools

import jax
import jax.numpy as jnp
from jax import lax
from jax.experimental import pallas as pl
from jax.experimental.pallas import tpu as pltpu
from jax.sharding import PartitionSpec as P


EPS = 1e-5
ROPE_BASE = 500000.0
NEG = -1e30
LOG2E = 1.4426950408889634

TOKENS = 128
DM = 3072
HEAD = 128
QPK = 3
LANES = QPK * TOKENS
HALF_KV = 4
HALF_Q = HALF_KV * QPK * HEAD
PAGE = 256
PAGES = 16
SLOTS = 8
GROUP = 4
META = GROUP * SLOTS + GROUP
FF = 8192
FF_HALF = FF // 2
DEPTH = 4
SCALE2 = HEAD ** -0.5 * LOG2E

MATE = [(0, 1), (1, 0), (2, 3), (3, 2)]
ACROSS = [(0, 2), (2, 0), (1, 3), (3, 1)]


def params(mb, sem=None):
    return pltpu.CompilerParams(vmem_limit_bytes=mb * 1024 * 1024, dimension_semantics=sem)


def f32dot(lhs, rhs):
    return jnp.dot(lhs, rhs, preferred_element_type=jnp.float32)


def normed(vals, gain):
    vals_f = vals.astype(jnp.float32)
    inv_rms = lax.rsqrt(jnp.mean(vals_f * vals_f, axis=-1, keepdims=True) + EPS)
    return (vals_f * inv_rms * gain.astype(jnp.float32)).astype(jnp.bfloat16)


def prep_body(me, page_ref, mine_ref, mate_ref, scr):
    core = me[0] % 2
    for kv in range(2):
        scr[kv] = page_ref[0, 0, kv].astype(jnp.float32).reshape(PAGE * 8, HEAD)
    for out_ref, half in ((mine_ref, core), (mate_ref, 1 - core)):
        for h in range(HALF_KV):
            rows = pl.ds(half * HALF_KV + h, PAGE, stride=8)
            out_ref[0, 0, h] = scr[0, rows, :].astype(jnp.bfloat16)
            val_t = scr[1, rows, :].T.astype(jnp.bfloat16)
            out_ref[0, 1, h, 0:128, :] = val_t[:, 0:128]
            out_ref[0, 1, h, 128:256, :] = val_t[:, 128:256]


def prep(me, pool, layer):
    shape = jax.ShapeDtypeStruct((PAGES, 2, HALF_KV, PAGE, HEAD), jnp.bfloat16)
    out_spec = pl.BlockSpec((1, 2, HALF_KV, PAGE, HEAD), lambda p, me: (p, 0, 0, 0, 0))
    return pl.pallas_call(
        prep_body,
        name="prep",
        out_shape=(shape, shape),
        grid_spec=pltpu.PrefetchScalarGridSpec(
            num_scalar_prefetch=1,
            grid=(PAGES,),
            in_specs=[pl.BlockSpec((1, 1, 2, PAGE, 8, HEAD), lambda p, me: (layer, p, 0, 0, 0, 0))],
            out_specs=[out_spec, out_spec],
            scratch_shapes=[pltpu.VMEM((2, PAGE * 8, HEAD), jnp.float32)],
        ),
        compiler_params=params(60, ("arbitrary",)),
        cost_estimate=pl.CostEstimate(flops=20_000_000_000, bytes_accessed=33_554_432, transcendentals=0),
    )(me, pool)


def rope_t(proj_t, cos_t, sin_t):
    first = proj_t[0:64]
    second = proj_t[64:128]
    return jnp.concatenate([first * cos_t - second * sin_t, second * cos_t + first * sin_t], axis=0)


def qkv_body(layer, with_kv, me, *refs):
    if with_kv:
        xa, xb, gain, cos_ref, sin_ref, wq, wk, wv, q_out, k_out, v_out, hx = refs
    else:
        xa, xb, gain, cos_ref, sin_ref, wq, q_out, hx = refs

    @pl.when(pl.program_id(0) == 0)
    def _():
        g = gain[layer:layer + 1, :]
        hx[0:TOKENS] = normed(xa[...], g)
        hx[TOKENS:2 * TOKENS] = normed(xb[...], g)

    cos_t = cos_ref[...]
    sin_t = sin_ref[...]
    hv = hx[...]
    q = f32dot(hv, wq[0])
    for r in range(2):
        for i in range(PAIR):
            for j in range(QPK):
                col = (i * QPK + j) * HEAD
                tile = q[r * TOKENS:(r + 1) * TOKENS, col:col + HEAD]
                q_out[r, i, :, j * TOKENS:(j + 1) * TOKENS] = rope_t(tile.T, cos_t, sin_t).astype(jnp.bfloat16)
    if with_kv:
        k = f32dot(hv, wk[0])
        v = f32dot(hv, wv[0])
        for r in range(2):
            for i in range(PAIR):
                part = (slice(r * TOKENS, (r + 1) * TOKENS), slice(i * HEAD, (i + 1) * HEAD))
                k_out[r, i] = rope_t(k[part].T, cos_t, sin_t).T.astype(jnp.bfloat16)
                v_out[r, i] = v[part].T.astype(jnp.bfloat16)


PAIR = 2


def qkv(me, layer, xa, xb, gain, cos_t, sin_t, wq, wk=None, wv=None):
    with_kv = wk is not None
    steps = HALF_KV // PAIR
    whole = lambda shape: pl.BlockSpec(shape, lambda h, me: (0,) * len(shape))
    cols = lambda width: pl.BlockSpec((1, DM, width), lambda h, me: (layer, 0, (me[0] % 2) * steps + h))
    in_specs = [whole((TOKENS, DM)), whole((TOKENS, DM)), whole((2, DM)), whole((64, TOKENS)), whole((64, TOKENS)), cols(PAIR * QPK * HEAD)]
    out_specs = [pl.BlockSpec((2, PAIR, HEAD, LANES), lambda h, me: (0, h, 0, 0))]
    out_shape = [jax.ShapeDtypeStruct((2, HALF_KV, HEAD, LANES), jnp.bfloat16)]
    args = [xa, xb, gain, cos_t, sin_t, wq]
    if with_kv:
        in_specs += [cols(PAIR * HEAD), cols(PAIR * HEAD)]
        out_specs += [pl.BlockSpec((2, PAIR, HEAD, HEAD), lambda h, me: (0, h, 0, 0))] * 2
        out_shape += [jax.ShapeDtypeStruct((2, HALF_KV, HEAD, HEAD), jnp.bfloat16)] * 2
        args += [wk, wv]
    flops = 2 * 2 * TOKENS * DM * (HALF_Q + (2 * HALF_KV * HEAD if with_kv else 0))
    return pl.pallas_call(
        functools.partial(qkv_body, layer, with_kv),
        name="qkv",
        out_shape=out_shape,
        grid_spec=pltpu.PrefetchScalarGridSpec(
            num_scalar_prefetch=1,
            grid=(steps,),
            in_specs=in_specs,
            out_specs=out_specs,
            scratch_shapes=[pltpu.VMEM((2 * TOKENS, DM), jnp.bfloat16)],
        ),
        compiler_params=params(40, ("arbitrary",)),
        cost_estimate=pl.CostEstimate(flops=flops, bytes_accessed=flops // 256, transcendentals=0),
    )(me, *args)


def attn_body(places, me_ref, meta, *refs):
    remote = places[0] >= 2
    first = places[0] % 2
    number = len(places)
    if remote:
        q_ref, kv_own, kv_mate, o_ref, buf, acc, ml, s_scr, mx_scr, sem = refs
    else:
        q_ref, k_new, v_new, kv_own, kv_mate, o_ref, buf, acc, ml, s_scr, mx_scr, sem = refs
    me = me_ref[0]
    core = me % 2
    mate = me + 1 - 2 * core
    across = me + 2 - 4 * (me // 2)
    by_place = (me, mate, across, across + 1 - 2 * core)
    reqs = [by_place[place] for place in places]
    n_own = [meta[place * META + GROUP * SLOTS + me] for place in places]
    n_req = [n_own[r] + meta[places[r] * META + GROUP * SLOTS + mate] for r in range(number)]
    total = sum(n_req[1:], n_req[0])

    def fetch(g):
        second = g >= n_req[0]
        t = jnp.where(second, g - n_req[0], g)
        own_count = jnp.where(second, n_own[-1], n_own[0])
        req = jnp.where(second, reqs[-1], reqs[0])
        is_own = t < own_count
        page = meta[jnp.where(is_own, 0, META) + req * SLOTS + jnp.where(is_own, t, t - own_count)]
        slot = g % DEPTH

        @pl.when(jnp.logical_and(g < total, is_own))
        def _():
            pltpu.make_async_copy(kv_own.at[page], buf.at[slot], sem.at[slot]).start()

        @pl.when(jnp.logical_and(g < total, jnp.logical_not(is_own)))
        def _():
            pltpu.make_async_copy(kv_mate.at[page], buf.at[slot], sem.at[slot]).start()

    def arrived(g):
        pltpu.make_async_copy(kv_own.at[0], buf.at[g % DEPTH], sem.at[g % DEPTH]).wait()

    for g in range(DEPTH - 1):
        @pl.when(g < total)
        def _():
            fetch(jnp.int32(g))

    def scores(r, h, slot, to):
        s = f32dot(buf[slot, 0, h], q_ref[first + r, h])
        s_scr[to] = s
        mx_scr[to] = jnp.max(s.reshape(PAGE // 8, 8, LANES), axis=0)

    def request(r, carry):
        count = jnp.where(r == 0, n_req[0], n_req[-1])
        base = jnp.where(r == 0, 0, n_req[0])
        for h in range(HALF_KV):
            if remote:
                acc[h] = jnp.zeros((HEAD, LANES), jnp.float32)
                ml[h, 0:1] = jnp.full((1, LANES), NEG, jnp.float32)
                ml[h, 1:2] = jnp.zeros((1, LANES), jnp.float32)
            else:
                s = f32dot(k_new[r, h], q_ref[r, h])
                key = lax.broadcasted_iota(jnp.int32, (TOKENS, LANES), 0)
                tok = lax.broadcasted_iota(jnp.int32, (TOKENS, LANES), 1) % TOKENS
                s = jnp.where(key <= tok, s, NEG)
                m = jnp.max(s, axis=0, keepdims=True)
                p = jnp.exp2((s - m) * SCALE2)
                ml[h, 0:1] = m
                ml[h, 1:2] = jnp.sum(p, axis=0, keepdims=True)
                acc[h] = f32dot(v_new[r, h], p.astype(jnp.bfloat16))

        @pl.when(count > 0)
        def _():
            arrived(base)
            scores(r, 0, base % DEPTH, 0)

        def unit(t, c):
            g = base + t
            slot = g % DEPTH
            fetch(g + DEPTH - 1)

            @pl.when(t + 1 < count)
            def _():
                arrived(g + 1)

            for h in range(HALF_KV):
                now = h % 2
                scores(r, (h + 1) % HALF_KV, slot if h + 1 < HALF_KV else (g + 1) % DEPTH, 1 - now)
                m_old = ml[h, 0:1]
                m = jnp.maximum(m_old, jnp.max(mx_scr[now], axis=0, keepdims=True))
                p = jnp.exp2((s_scr[now] - m) * SCALE2)
                keep = jnp.exp2((m_old - m) * SCALE2)
                ml[h, 0:1] = m
                ml[h, 1:2] = ml[h, 1:2] * keep + jnp.sum(p, axis=0, keepdims=True)
                val_t = jnp.concatenate([buf[slot, 1, h, 0:128, :], buf[slot, 1, h, 128:256, :]], axis=1)
                acc[h] = acc[h] * keep + f32dot(val_t, p.astype(jnp.bfloat16))
            return c

        lax.fori_loop(0, count, unit, 0)
        for h in range(HALF_KV):
            o_ref[r, h * HEAD:(h + 1) * HEAD] = acc[h]
            o_ref[r, ROWS_O + h:ROWS_O + h + 1] = ml[h, 0:1]
            o_ref[r, ROWS_O + HALF_KV + h:ROWS_O + HALF_KV + h + 1] = ml[h, 1:2]
        return carry

    lax.fori_loop(0, number, request, 0)


ROWS_O = HALF_KV * HEAD
ROWS = ROWS_O + 2 * HALF_KV


def attn(places, me, meta, q, kv_own, kv_mate, k_new=None, v_new=None):
    vmem = pl.BlockSpec(memory_space=pltpu.VMEM)
    hbm = pl.BlockSpec(memory_space=pltpu.HBM)
    args = [q] if k_new is None else [q, k_new, v_new]
    number = len(places)
    return pl.pallas_call(
        functools.partial(attn_body, places),
        name="attn",
        out_shape=jax.ShapeDtypeStruct((number, ROWS, LANES), jnp.float32),
        grid_spec=pltpu.PrefetchScalarGridSpec(
            num_scalar_prefetch=2,
            grid=(),
            in_specs=[vmem] * len(args) + [hbm, hbm],
            out_specs=vmem,
            scratch_shapes=[
                pltpu.VMEM((DEPTH, 2, HALF_KV, PAGE, HEAD), jnp.bfloat16),
                pltpu.VMEM((HALF_KV, HEAD, LANES), jnp.float32),
                pltpu.VMEM((HALF_KV, 8, LANES), jnp.float32),
                pltpu.VMEM((2, PAGE, LANES), jnp.float32),
                pltpu.VMEM((2, 8, LANES), jnp.float32),
                pltpu.SemaphoreType.DMA((DEPTH,)),
            ],
        ),
        compiler_params=params(56),
        cost_estimate=pl.CostEstimate(flops=8_000_000_000 * number, bytes_accessed=5_000_000 * number, transcendentals=0),
    )(me, meta, *args, kv_own, kv_mate)


def merge_body(loc, rem_a, rem_b, a_ref):
    for r, rem in enumerate((rem_a, rem_b)):
        for h in range(HALF_KV):
            top, mid = ROWS_O + h, ROWS_O + HALF_KV + h
            m1, l1 = loc[r, top:top + 1], loc[r, mid:mid + 1]
            m2, l2 = rem[0, top:top + 1], rem[0, mid:mid + 1]
            m = jnp.maximum(m1, m2)
            w1 = jnp.exp2((m1 - m) * SCALE2)
            w2 = jnp.exp2((m2 - m) * SCALE2)
            inv = 1.0 / (l1 * w1 + l2 * w2)
            rows = slice(h * HEAD, (h + 1) * HEAD)
            out = loc[r, rows] * (w1 * inv) + rem[0, rows] * (w2 * inv)
            for j in range(QPK):
                col = (h * QPK + j) * HEAD
                a_ref[r, :, col:col + HEAD] = out[:, j * TOKENS:(j + 1) * TOKENS].T.astype(jnp.bfloat16)


def merge(loc, rem_a, rem_b):
    vmem = pl.BlockSpec(memory_space=pltpu.VMEM)
    return pl.pallas_call(
        merge_body,
        name="merge",
        out_shape=jax.ShapeDtypeStruct((2, TOKENS, HALF_Q), jnp.bfloat16),
        in_specs=[vmem] * 3,
        out_specs=vmem,
        compiler_params=params(16),
        cost_estimate=pl.CostEstimate(flops=1_000_000_000, bytes_accessed=4_000_000, transcendentals=0),
    )(loc, rem_a, rem_b)


WO_BLK = 512
WO_STEPS = DM // WO_BLK
FF_BLK = 256
FF_STEPS = FF_HALF // FF_BLK
DOWN_BLK = 512


def post_body(layer, me, a_own, a_mate, xa, xb, gain, wo, wg, wu, wd, base_ref, send_ref, a_scr, x1, h2):
    core = me[0] % 2
    n = pl.program_id(0)

    @pl.when(n == 0)
    def _():
        own = pl.ds(pl.multiple_of(core * HALF_Q, HALF_Q), HALF_Q)
        other = pl.ds(pl.multiple_of((1 - core) * HALF_Q, HALF_Q), HALF_Q)
        a_scr[0:TOKENS, own] = a_own[0]
        a_scr[TOKENS:2 * TOKENS, own] = a_own[1]
        a_scr[0:TOKENS, other] = a_mate[1]
        a_scr[TOKENS:2 * TOKENS, other] = a_mate[0]

    @pl.when(n < WO_STEPS)
    def _():
        prod = f32dot(a_scr[...], wo[0])
        cols = pl.ds(pl.multiple_of(n * WO_BLK, WO_BLK), WO_BLK)
        x1[0:TOKENS, cols] = (xa[...].astype(jnp.float32) + prod[0:TOKENS]).astype(jnp.bfloat16)
        x1[TOKENS:2 * TOKENS, cols] = (xb[...].astype(jnp.float32) + prod[TOKENS:]).astype(jnp.bfloat16)

    @pl.when(n == WO_STEPS - 1)
    def _():
        h2[...] = normed(x1[...], gain[layer:layer + 1, :])

    @pl.when(n >= WO_STEPS)
    def _():
        first = n == WO_STEPS
        hv = h2[...]
        gate = f32dot(hv, wg[0])
        up = f32dot(hv, wu[0])
        gated = (jax.nn.silu(gate) * up).astype(jnp.bfloat16)
        for d in range(DM // DOWN_BLK):
            cols = slice(d * DOWN_BLK, (d + 1) * DOWN_BLK)
            y = f32dot(gated, wd[0, :, cols])
            base_ref[:, cols] = jnp.where(first, x1[0:TOKENS, cols].astype(jnp.float32), base_ref[:, cols]) + y[0:TOKENS]
            send_ref[:, cols] = jnp.where(first, 0.0, send_ref[:, cols]) + y[TOKENS:]


def post(me, layer, a_own, a_mate, xa, xb, gain, wo, wg, wu, wd):
    whole = lambda shape: pl.BlockSpec(shape, lambda n, me: (0,) * len(shape))
    early = lambda n: jnp.minimum(n, WO_STEPS - 1)
    late = lambda n, me: (me[0] % 2) * FF_STEPS + jnp.maximum(n - WO_STEPS, 0)
    x_spec = pl.BlockSpec((TOKENS, WO_BLK), lambda n, me: (0, early(n)))
    cols = pl.BlockSpec((1, DM, FF_BLK), lambda n, me: (layer, 0, late(n, me)))
    rows = pl.BlockSpec((1, FF_BLK, DM), lambda n, me: (layer, late(n, me), 0))
    shape = jax.ShapeDtypeStruct((TOKENS, DM), jnp.float32)
    act = pltpu.VMEM((2 * TOKENS, DM), jnp.bfloat16)
    return pl.pallas_call(
        functools.partial(post_body, layer),
        name="post",
        out_shape=(shape, shape),
        grid_spec=pltpu.PrefetchScalarGridSpec(
            num_scalar_prefetch=1,
            grid=(WO_STEPS + FF_STEPS,),
            in_specs=[
                whole((2, TOKENS, HALF_Q)), whole((2, TOKENS, HALF_Q)), x_spec, x_spec, whole((2, DM)),
                pl.BlockSpec((1, DM, WO_BLK), lambda n, me: (layer, 0, early(n))), cols, cols, rows,
            ],
            out_specs=[whole((TOKENS, DM)), whole((TOKENS, DM))],
            scratch_shapes=[act, act, act],
        ),
        compiler_params=params(48, ("arbitrary",)),
        cost_estimate=pl.CostEstimate(flops=24_000_000_000, bytes_accessed=95_000_000, transcendentals=0),
    )(me, a_own, a_mate, xa, xb, gain, wo, wg, wu, wd)


def solution(mesh):
    by_request = P(('replica', 'pool'))
    by_owner = P(None, ('replica', 'pool'))
    shared = P()

    def per_device(pool_loc, idx_loc, count_loc, x_loc, norm_attn, wq, wk, wv, wo, norm_mlp, w_gate, w_up, w_down):
        layers = pool_loc.shape[0]
        to_mate = lambda arr: lax.ppermute(arr, 'pool', MATE)
        to_across = lambda arr: lax.ppermute(arr, 'pool', ACROSS)
        me = lax.axis_index('pool').astype(jnp.int32).reshape(1)
        row = jnp.concatenate([idx_loc.reshape(-1), count_loc.reshape(-1)]).reshape(1, META)
        chip = jnp.concatenate([row, to_mate(row)])
        meta = jnp.concatenate([chip, to_across(chip)]).reshape(GROUP * META)
        half = HEAD // 2
        freqs = ROPE_BASE ** (-jnp.arange(half, dtype=jnp.float32) / half)
        angles = freqs[:, None] * jnp.arange(TOKENS, dtype=jnp.float32)[None, :]
        cos_t = jnp.cos(angles)
        sin_t = jnp.sin(angles)
        x = x_loc[0]
        for layer in range(layers):
            x_across = to_across(x)
            x_mate = to_mate(x)
            kv_own, kv_give = prep(me, pool_loc, layer)
            kv_mate = to_mate(kv_give)
            x_diag = to_mate(x_across)
            q_far, = qkv(me, layer, x_across, x_diag, norm_attn, cos_t, sin_t, wq)
            part_a = attn((2,), me, meta, q_far, kv_own, kv_mate)
            got_a = to_across(part_a)
            part_b = attn((3,), me, meta, q_far, kv_own, kv_mate)
            got_b = to_across(part_b)
            q_near, k_new, v_new = qkv(me, layer, x, x_mate, norm_attn, cos_t, sin_t, wq, wk, wv)
            part = attn((0, 1), me, meta, q_near, kv_own, kv_mate, k_new, v_new)
            a_own = merge(part, got_a, got_b)
            a_mate = to_mate(a_own)
            base, y_send = post(me, layer, a_own, a_mate, x, x_mate, norm_mlp, wo, w_gate, w_up, w_down)
            y_got = to_mate(y_send)
            x = (base + y_got).astype(jnp.bfloat16)
        return x[None]

    return jax.shard_map(per_device, mesh=mesh, in_specs=(by_owner, by_owner, by_request, by_request, shared, shared, shared, shared, shared, shared, shared, shared, shared), out_specs=by_request, check_vma=False)
```

time: 370 us -> 310 us (0.84)
  Pallas kernels: 281 us -> 203 us
  starting transfers between devices: 9.36 us -> 35 us
  local copies, waits for them, and re-layouts: 18 us -> 7.57 us
  waiting for transfers between devices: 49.7 us -> 58.9 us
  blocking collectives: 5.15 us -> 0 us
    pallas_call x8, Pallas kernels: 203 us -> 131 us  [the longest x2 91.8 us: post(): pl.pallas_call(functools.partial(post_body, layer), name='post', out_shap...]
    ppermute x6 -> x7, starting transfers between devices: 5.29 us -> 31.2 us  [per_device(): to_across = lambda arr: lax.ppermute(arr, 'pool', ACROSS)]
    unnamed x33 -> x31, local copies, waits for them, and re-layouts: 17.9 us -> 6.8 us
    ppermute x6 -> x7, waiting for transfers between devices: 38 us -> 48.5 us  [per_device(): to_across = lambda arr: lax.ppermute(arr, 'pool', ACROSS)]
    pallas_call x4, Pallas kernels: 37.5 us -> 31.6 us  [qkv(): pl.pallas_call(functools.partial(qkv_body, layer, with_kv), name='qkv', o...]
    unnamed x1 -> x0, blocking collectives: 5.15 us -> none
    ppermute x10 -> x11, waiting for transfers between devices: 11.7 us -> 10.5 us  [per_device(): to_mate = lambda arr: lax.ppermute(arr, 'pool', MATE)]
  transfers between devices with their start and end apart: 16 -> 18, of which waited for: 7 -> 8; matrix products, arithmetic and copies ran while one was open for 1% -> 1% of each run, Pallas kernels for 58% -> 43%
where the time goes in v2:
time: 310 us; the launch traced here: 307 us
  Pallas kernels  203 us (65%)
  waiting for transfers between devices  58.9 us (19%)
  starting transfers between devices  35 us (11%)
  local copies, waits for them, and re-layouts  7.57 us (2%)
    pallas_call x2, Pallas kernels, post(): pl.pallas_call(functools.partial(post_body, layer), name='post', out_shap...  91.8 us
    ppermute x7, waiting for transfers between devices, per_device(): to_across = lambda arr: lax.ppermute(arr, 'pool', ACROSS)  48.5 us
    pallas_call x2, Pallas kernels, prep(): pl.pallas_call(prep_body, name='prep', out_shape=(shape, shape), grid_spe...  39.7 us
    pallas_call x6, Pallas kernels, attn(): pl.pallas_call(functools.partial(attn_body, places), name='attn', out_sha...  39.4 us
    pallas_call x4, Pallas kernels, qkv(): pl.pallas_call(functools.partial(qkv_body, layer, with_kv), name='qkv', o...  31.6 us
    ppermute x7, starting transfers between devices, per_device(): to_across = lambda arr: lax.ppermute(arr, 'pool', ACROSS)  31.2 us
    ppermute x11, waiting for transfers between devices, per_device(): to_mate = lambda arr: lax.ppermute(arr, 'pool', MATE)  10.5 us
    unnamed x31, local copies, waits for them, and re-layouts  6.8 us
  transfers between devices with their start and end apart: 18, of which 8 were waited for; matrix products, arithmetic and copies ran while one was open for 1% of the time, Pallas kernels for 43%

profile of v2, /device:TPU:0, one launch (start us, length us, event | category | flops | bytes accessed | tf_op | source)
XLA Modules:
  0.0 307.3 jit_solution(17354581255581951273)
XLA Ops:
  0.0 19.8 %prep.2 = (bf16[16,2,4,256,128]{4,3,2,1,0:T(8,128)(2,1)}, bf16[16,2,4,256,128]{4,3,2,1,0:T(8,128)(2,1)}) custom-call(s32[1]{0:T(128)} %bitcast.me.me_ref, bf16[2,16,2,256,8,128]{5,4,3,2,1,0:T(8,128)(2,1)} %page_ref.3), custom_call_target="tpu_custom_call" | custom-call | flops 20000000000 | bytes 33554432 | tf_op jit(solution)/shard_map/prep/pallas_call | solution.py:67
  24.9 19.9 %prep.3 = (bf16[16,2,4,256,128]{4,3,2,1,0:T(8,128)(2,1)}, bf16[16,2,4,256,128]{4,3,2,1,0:T(8,128)(2,1)}) custom-call(s32[1]{0:T(128)} %bitcast.me.me_ref, bf16[2,16,2,256,8,128]{5,4,3,2,1,0:T(8,128)(2,1)} %page_ref.3), custom_call_target="tpu_custom_call" | custom-call | flops 20000000000 | bytes 33554432 | tf_op jit(solution)/shard_map/prep/pallas_call | solution.py:67
  45.6 3.3 %collective-permute-done.1 = s32[2,36]{1,0:T(2,128)S(1)} collective-permute-done((s32[2,36]{1,0:T(2,128)S(1)}, s32[2,36]{1,0:T(2,128)S(1)}, u32[]{:S(2)}, u32[]{:S(2)}) %collective-permute-start.1) | collective-permute-done | bytes 320 | tf_op jit(solution)/shard_map/ppermute | solution.py:402
  49.7 9.2 %qkv.4 = (bf16[2,4,128,384]{3,2,1,0:T(8,128)(2,1)S(1)}, bf16[2,4,128,128]{3,2,1,0:T(8,128)(2,1)S(1)}, bf16[2,4,128,128]{3,2,1,0:T(8,128)(2,1)S(1)}) custom-call(s32[1]{0:T(128)} %bitcast.me.me_ref, bf16[128,3072]{1,0:T(8,128)(2,1)S(1)} %bitcast.9, bf16[128,3072]{1,0:T(8,128)(2,1)S(1)} %collective-permute-done.2.refs_1_.xb, bf16[2,3072]{1,0:T(2,128)(2,1)S(1)} %copy-done.5, ...), custom_call_target="tpu_custom_call" | custom-call | flops 4026531840 | bytes 15728640 | tf_op jit(solution)/shard_map/qkv/pallas_call | solution.py:139
  60.4 6.5 %qkv.5.refs_0_ = bf16[2,4,128,384]{3,2,1,0:T(8,128)(2,1)S(1)} custom-call(s32[1]{0:T(128)} %bitcast.me.me_ref, bf16[128,3072]{1,0:T(8,128)(2,1)S(1)} %collective-permute-done.4.refs_0_, bf16[128,3072]{1,0:T(8,128)(2,1)S(1)} %collective-permute-done.5.refs_1_, bf16[2,3072]{1,0:T(2,128)(2,1)S(1)} %copy-done.5, f32[64,128]{1,0:T(8,128)S(1)} %get-tuple-element.34.refs_3_, ...), custom_call_target="tpu_custom_call" | custom-call | flops 2415919104 | bytes 9437184 | tf_op jit(solution)/shard_map/qkv/pallas_call | solution.py:139
  67.8 4.8 %attn.8 = f32[1,520,384]{2,1,0:T(8,128)} custom-call(s32[1]{0:T(128)} %bitcast.me.me_ref, s32[144]{0:T(256)} %reshape.25.meta, bf16[2,4,128,384]{3,2,1,0:T(8,128)(2,1)} %copy-done.4, bf16[16,2,4,256,128]{4,3,2,1,0:T(8,128)(2,1)} %get-tuple-element.22.refs_3_.refs_1_, bf16[16,2,4,256,128]{4,3,2,1,0:T(8,128)(2,1)} %collective-permute-done.3.refs_4_.refs_2_), custom_call_target="tpu_custom_call" | custom-call | flops 8000000000 | bytes 5000000 | tf_op jit(solution)/shard_map/attn/pallas_call | solution.py:268
  72.7 5.7 %collective-permute-start.7 = (f32[1,520,384]{2,1,0:T(8,128)}, f32[1,520,384]{2,1,0:T(8,128)S(1)}, u32[]{:S(2)}, u32[]{:S(2)}) collective-permute-start(f32[1,520,384]{2,1,0:T(8,128)} %attn.8), channel_id=1, source_target_pairs={{0,2},{2,0},{1,3},{3,1},{4,6},{6,4},{5,7},{7,5},{8,10},{10,8},{9,1... | collective-permute-start | bytes 2396168 | tf_op jit(solution)/shard_map/ppermute | solution.py:402
  78.3 5.8 %attn.7 = f32[1,520,384]{2,1,0:T(8,128)} custom-call(s32[1]{0:T(128)} %bitcast.me.me_ref, s32[144]{0:T(256)} %reshape.25.meta, bf16[2,4,128,384]{3,2,1,0:T(8,128)(2,1)} %copy-done.4, bf16[16,2,4,256,128]{4,3,2,1,0:T(8,128)(2,1)} %get-tuple-element.22.refs_3_.refs_1_, bf16[16,2,4,256,128]{4,3,2,1,0:T(8,128)(2,1)} %collective-permute-done.3.refs_4_.refs_2_), custom_call_target="tpu_custom_call" | custom-call | flops 8000000000 | bytes 5000000 | tf_op jit(solution)/shard_map/attn/pallas_call | solution.py:268
  84.2 6.4 %collective-permute-start.6 = (f32[1,520,384]{2,1,0:T(8,128)}, f32[1,520,384]{2,1,0:T(8,128)S(1)}, u32[]{:S(2)}, u32[]{:S(2)}) collective-permute-start(f32[1,520,384]{2,1,0:T(8,128)} %attn.7), channel_id=1, source_target_pairs={{0,2},{2,0},{1,3},{3,1},{4,6},{6,4},{5,7},{7,5},{8,10},{10,8},{9,1... | collective-permute-start | bytes 2396168 | tf_op jit(solution)/shard_map/ppermute | solution.py:402
  90.6 9.1 %attn.6.loc = f32[2,520,384]{2,1,0:T(8,128)} custom-call(s32[1]{0:T(128)} %bitcast.me.me_ref, s32[144]{0:T(256)} %reshape.25.meta, bf16[2,4,128,384]{3,2,1,0:T(8,128)(2,1)} %copy-done.8, bf16[2,4,128,128]{3,2,1,0:T(8,128)(2,1)} %copy-done.11, bf16[2,4,128,128]{3,2,1,0:T(8,128)(2,1)} %copy-done.12, ...), custom_call_target="tpu_custom_call" | custom-call | flops 16000000000 | bytes 10000000 | tf_op jit(solution)/shard_map/attn/pallas_call | solution.py:268
  99.7 14.1 %collective-permute-done.6.rem_a = f32[1,520,384]{2,1,0:T(8,128)S(1)} collective-permute-done((f32[1,520,384]{2,1,0:T(8,128)}, f32[1,520,384]{2,1,0:T(8,128)S(1)}, u32[]{:S(2)}, u32[]{:S(2)}) %collective-permute-start.6) | collective-permute-done | bytes 798752 | tf_op jit(solution)/shard_map/ppermute | solution.py:402
  118.0 45.9 %post.2 = (f32[128,3072]{1,0:T(8,128)S(1)}, f32[128,3072]{1,0:T(8,128)}) custom-call(s32[1]{0:T(128)} %bitcast.me.me_ref, bf16[2,128,1536]{2,1,0:T(8,128)(2,1)S(1)} %merge.2.a_own, bf16[2,128,1536]{2,1,0:T(8,128)(2,1)S(1)} %collective-permute-done.8.a_mate, bf16[128,3072]{1,0:T(8,128)(2,1)S(1)} %bitcast.10, ...), custom_call_target="tpu_custom_call" | custom-call | flops 24000000000 | bytes 95000000 | tf_op jit(solution)/shard_map/post/pallas_call | solution.py:375
  164.2 3.3 %collective-permute-done.9 = f32[128,3072]{1,0:T(8,128)S(1)} collective-permute-done((f32[128,3072]{1,0:T(8,128)}, f32[128,3072]{1,0:T(8,128)S(1)}, u32[]{:S(2)}, u32[]{:S(2)}) %collective-permute-start.9) | collective-permute-done | bytes 1572896 | tf_op jit(solution)/shard_map/ppermute | solution.py:401
  170.0 17.8 %collective-permute-done.12.refs_0_ = bf16[128,3072]{1,0:T(8,128)(2,1)S(1)} collective-permute-done((bf16[128,3072]{1,0:T(8,128)(2,1)S(1)}, bf16[128,3072]{1,0:T(8,128)(2,1)S(1)}, u32[]{:S(2)}, u32[]{:S(2)}) %collective-permute-start.12) | collective-permute-done | bytes 786464 | tf_op jit(solution)/shard_map/ppermute | solution.py:402
  187.9 9.2 %qkv.6 = (bf16[2,4,128,384]{3,2,1,0:T(8,128)(2,1)S(1)}, bf16[2,4,128,128]{3,2,1,0:T(8,128)(2,1)S(1)}, bf16[2,4,128,128]{3,2,1,0:T(8,128)(2,1)S(1)}) custom-call(s32[1]{0:T(128)} %bitcast.me.me_ref, bf16[128,3072]{1,0:T(8,128)(2,1)S(1)} %add_convert_fusion.1.refs_0_.xa, bf16[128,3072]{1,0:T(8,128)(2,1)S(1)} %collective-permute-done.10.refs_1_.xb, ...), custom_call_target="tpu_custom_call" | custom-call | flops 4026531840 | bytes 15728640 | tf_op jit(solution)/shard_map/qkv/pallas_call | solution.py:139
  197.1 6.8 %qkv.7.refs_0_ = bf16[2,4,128,384]{3,2,1,0:T(8,128)(2,1)S(1)} custom-call(s32[1]{0:T(128)} %bitcast.me.me_ref, bf16[128,3072]{1,0:T(8,128)(2,1)S(1)} %collective-permute-done.12.refs_0_, bf16[128,3072]{1,0:T(8,128)(2,1)S(1)} %collective-permute-done.13.refs_1_, bf16[2,3072]{1,0:T(2,128)(2,1)S(1)} %copy-done.5, f32[64,128]{1,0:T(8,128)S(1)} %get-tuple-element.34.refs_3_, ...), custom_call_target="tpu_custom_call" | custom-call | flops 2415919104 | bytes 9437184 | tf_op jit(solution)/shard_map/qkv/pallas_call | solution.py:139
  204.9 4.9 %attn.11 = f32[1,520,384]{2,1,0:T(8,128)} custom-call(s32[1]{0:T(128)} %bitcast.me.me_ref, s32[144]{0:T(256)} %reshape.25.meta, bf16[2,4,128,384]{3,2,1,0:T(8,128)(2,1)} %copy-done.3, bf16[16,2,4,256,128]{4,3,2,1,0:T(8,128)(2,1)} %get-tuple-element.29.refs_3_.refs_1_, bf16[16,2,4,256,128]{4,3,2,1,0:T(8,128)(2,1)} %collective-permute-done.11.refs_4_.refs_2_), custom_call_target="tpu_custom_call" | custom-call | flops 8000000000 | bytes 5000000 | tf_op jit(solution)/shard_map/attn/pallas_call | solution.py:268
  209.7 7.3 %collective-permute-start.15 = (f32[1,520,384]{2,1,0:T(8,128)}, f32[1,520,384]{2,1,0:T(8,128)S(1)}, u32[]{:S(2)}, u32[]{:S(2)}) collective-permute-start(f32[1,520,384]{2,1,0:T(8,128)} %attn.11), channel_id=1, source_target_pairs={{0,2},{2,0},{1,3},{3,1},{4,6},{6,4},{5,7},{7,5},{8,10},{10,8},{9,1... | collective-permute-start | bytes 2396168 | tf_op jit(solution)/shard_map/ppermute | solution.py:402
  217.1 5.9 %attn.10 = f32[1,520,384]{2,1,0:T(8,128)} custom-call(s32[1]{0:T(128)} %bitcast.me.me_ref, s32[144]{0:T(256)} %reshape.25.meta, bf16[2,4,128,384]{3,2,1,0:T(8,128)(2,1)} %copy-done.3, bf16[16,2,4,256,128]{4,3,2,1,0:T(8,128)(2,1)} %get-tuple-element.29.refs_3_.refs_1_, bf16[16,2,4,256,128]{4,3,2,1,0:T(8,128)(2,1)} %collective-permute-done.11.refs_4_.refs_2_), custom_call_target="tpu_custom_call" | custom-call | flops 8000000000 | bytes 5000000 | tf_op jit(solution)/shard_map/attn/pallas_call | solution.py:268
  223.0 6.4 %collective-permute-start.14 = (f32[1,520,384]{2,1,0:T(8,128)}, f32[1,520,384]{2,1,0:T(8,128)S(1)}, u32[]{:S(2)}, u32[]{:S(2)}) collective-permute-start(f32[1,520,384]{2,1,0:T(8,128)} %attn.10), channel_id=1, source_target_pairs={{0,2},{2,0},{1,3},{3,1},{4,6},{6,4},{5,7},{7,5},{8,10},{10,8},{9,1... | collective-permute-start | bytes 2396168 | tf_op jit(solution)/shard_map/ppermute | solution.py:402
  229.4 9.0 %attn.9.loc = f32[2,520,384]{2,1,0:T(8,128)} custom-call(s32[1]{0:T(128)} %bitcast.me.me_ref, s32[144]{0:T(256)} %reshape.25.meta, bf16[2,4,128,384]{3,2,1,0:T(8,128)(2,1)} %copy-done.7, bf16[2,4,128,128]{3,2,1,0:T(8,128)(2,1)} %copy-done.9, bf16[2,4,128,128]{3,2,1,0:T(8,128)(2,1)} %copy-done.10, ...), custom_call_target="tpu_custom_call" | custom-call | flops 16000000000 | bytes 10000000 | tf_op jit(solution)/shard_map/attn/pallas_call | solution.py:268
  238.4 13.2 %collective-permute-done.14.rem_a = f32[1,520,384]{2,1,0:T(8,128)S(1)} collective-permute-done((f32[1,520,384]{2,1,0:T(8,128)}, f32[1,520,384]{2,1,0:T(8,128)S(1)}, u32[]{:S(2)}, u32[]{:S(2)}) %collective-permute-start.14) | collective-permute-done | bytes 798752 | tf_op jit(solution)/shard_map/ppermute | solution.py:402
  256.7 45.9 %post.3 = (f32[128,3072]{1,0:T(8,128)S(1)}, f32[128,3072]{1,0:T(8,128)}) custom-call(s32[1]{0:T(128)} %bitcast.me.me_ref, bf16[2,128,1536]{2,1,0:T(8,128)(2,1)S(1)} %merge.3.a_own, bf16[2,128,1536]{2,1,0:T(8,128)(2,1)S(1)} %collective-permute-done.16.a_mate, bf16[128,3072]{1,0:T(8,128)(2,1)S(1)} %add_convert_fusion.1.refs_0_.xa, ...), custom_call_target="tpu_custom_call" | custom-call | flops 24000000000 | bytes 95000000 | tf_op jit(solution)/shard_map/post/pallas_call | solution.py:375
  303.0 3.2 %collective-permute-done.17 = f32[128,3072]{1,0:T(8,128)S(1)} collective-permute-done((f32[128,3072]{1,0:T(8,128)}, f32[128,3072]{1,0:T(8,128)S(1)}, u32[]{:S(2)}, u32[]{:S(2)}) %collective-permute-start.17) | collective-permute-done | bytes 1572896 | tf_op jit(solution)/shard_map/ppermute | solution.py:401
  (69 shorter events, 23.6 us)
Async XLA Ops:
  0.0 20.6 %copy-start = (bf16[1,128,3072]{2,1,0:T(8,128)(2,1)S(1)}, bf16[1,128,3072]{2,1,0:T(8,128)(2,1)}, u32[]{:S(2)}) copy-start(bf16[1,128,3072]{2,1,0:T(8,128)(2,1)} %param.16) | copy-start | bytes 2359300
  0.0 24.1 %copy-start.13 = (s32[4,1,8]{2,1,0:T(1,128)S(1)}, s32[4,1,8]{2,1,0:T(1,128)}, u32[]{:S(2)}) copy-start(s32[4,1,8]{2,1,0:T(1,128)} %param.14) | copy-start | bytes 388
  0.0 24.8 %copy-start.14 = (s32[1,4]{1,0:T(1,128)S(1)}, s32[1,4]{1,0:T(1,128)}, u32[]{:S(2)}) copy-start(s32[1,4]{1,0:T(1,128)} %param.15) | copy-start | bytes 52
  19.8 48.0 %collective-permute-start.3 = (bf16[16,2,4,256,128]{4,3,2,1,0:T(8,128)(2,1)}, bf16[16,2,4,256,128]{4,3,2,1,0:T(8,128)(2,1)}, u32[]{:S(2)}, u32[]{:S(2)}) collective-permute-start(bf16[16,2,4,256,128]{4,3,2,1,0:T(8,128)(2,1)} %get-tuple-element.23), channel_id=1, source_target_pairs={{0,1},{1,0},{2,3},{3,2},{4,5},{5,4},{6,7},{7,6},{8,9},{9,8},{10,11... | collective-permute-start | bytes 25165832 | tf_op jit(solution)/shard_map/ppermute | solution.py:401
  20.6 29.1 %collective-permute-start.2 = (bf16[128,3072]{1,0:T(8,128)(2,1)S(1)}, bf16[128,3072]{1,0:T(8,128)(2,1)S(1)}, u32[]{:S(2)}, u32[]{:S(2)}) collective-permute-start(bf16[128,3072]{1,0:T(8,128)(2,1)S(1)} %bitcast.7), channel_id=1, source_target_pairs={{0,1},{1,0},{2,3},{3,2},{4,5},{5,4},{6,7},{7,6},{8,9},{9,8},{10,11... | collective-permute-start | bytes 2359304 | tf_op jit(solution)/shard_map/ppermute | solution.py:401
  20.6 24.6 %collective-permute-start.4 = (bf16[128,3072]{1,0:T(8,128)(2,1)S(1)}, bf16[128,3072]{1,0:T(8,128)(2,1)S(1)}, u32[]{:S(2)}, u32[]{:S(2)}) collective-permute-start(bf16[128,3072]{1,0:T(8,128)(2,1)S(1)} %bitcast.8), channel_id=1, source_target_pairs={{0,2},{2,0},{1,3},{3,1},{4,6},{6,4},{5,7},{7,5},{8,10},{10,8},{9,1... | collective-permute-start | bytes 2359304 | tf_op jit(solution)/shard_map/ppermute | solution.py:402
  24.9 24.8 %copy-start.5 = (bf16[2,3072]{1,0:T(2,128)(2,1)S(1)}, bf16[2,3072]{1,0:T(2,128)(2,1)}, u32[]{:S(2)}) copy-start(bf16[2,3072]{1,0:T(2,128)(2,1)} %refs_2_.7) | copy-start | bytes 36868
  24.9 20.5 %collective-permute-start = (s32[1,36]{1,0:T(1,128)S(1)}, s32[1,36]{1,0:T(1,128)S(1)}, u32[]{:S(2)}, u32[]{:S(2)}) collective-permute-start(s32[1,36]{1,0:T(1,128)S(1)} %add_bitcast_fusion), channel_id=1, source_target_pairs={{0,1},{1,0},{2,3},{3,2},{4,5},{5,4},{6,7},{7,6},{8,9},{9,8},{10,11... | collective-permute-start | bytes 440 | tf_op jit(solution)/shard_map/ppermute | solution.py:401
  44.8 160.1 %collective-permute-start.11 = (bf16[16,2,4,256,128]{4,3,2,1,0:T(8,128)(2,1)}, bf16[16,2,4,256,128]{4,3,2,1,0:T(8,128)(2,1)}, u32[]{:S(2)}, u32[]{:S(2)}) collective-permute-start(bf16[16,2,4,256,128]{4,3,2,1,0:T(8,128)(2,1)} %get-tuple-element.30), channel_id=1, source_target_pairs={{0,1},{1,0},{2,3},{3,2},{4,5},{5,4},{6,7},{7,6},{8,9},{9,8},{10,11... | collective-permute-start | bytes 25165832 | tf_op jit(solution)/shard_map/ppermute | solution.py:401
  45.3 15.1 %collective-permute-start.5 = (bf16[128,3072]{1,0:T(8,128)(2,1)S(1)}, bf16[128,3072]{1,0:T(8,128)(2,1)S(1)}, u32[]{:S(2)}, u32[]{:S(2)}) collective-permute-start(bf16[128,3072]{1,0:T(8,128)(2,1)S(1)} %collective-permute-done.4.refs_0_), channel_id=1, source_target_pairs={{0,1},{1,0},{2,3},{3,2},{4,5},{5,4},{6,7},{7,6},{8,9},{9,8},{10,11... | collective-permute-start | bytes 2359304 | tf_op jit(solution)/shard_map/ppermute | solution.py:401
  45.4 3.6 %collective-permute-start.1 = (s32[2,36]{1,0:T(2,128)S(1)}, s32[2,36]{1,0:T(2,128)S(1)}, u32[]{:S(2)}, u32[]{:S(2)}) collective-permute-start(s32[2,36]{1,0:T(2,128)S(1)} %pad_add_fusion.1), channel_id=1, source_target_pairs={{0,2},{2,0},{1,3},{3,1},{4,6},{6,4},{5,7},{7,5},{8,10},{10,8},{9,1... | collective-permute-start | bytes 872 | tf_op jit(solution)/shard_map/ppermute | solution.py:402
  72.7 27.0 %collective-permute-start.7 = (f32[1,520,384]{2,1,0:T(8,128)}, f32[1,520,384]{2,1,0:T(8,128)S(1)}, u32[]{:S(2)}, u32[]{:S(2)}) collective-permute-start(f32[1,520,384]{2,1,0:T(8,128)} %attn.8), channel_id=1, source_target_pairs={{0,2},{2,0},{1,3},{3,1},{4,6},{6,4},{5,7},{7,5},{8,10},{10,8},{9,1... | collective-permute-start | bytes 2396168 | tf_op jit(solution)/shard_map/ppermute | solution.py:402
  84.2 29.7 %collective-permute-start.6 = (f32[1,520,384]{2,1,0:T(8,128)}, f32[1,520,384]{2,1,0:T(8,128)S(1)}, u32[]{:S(2)}, u32[]{:S(2)}) collective-permute-start(f32[1,520,384]{2,1,0:T(8,128)} %attn.7), channel_id=1, source_target_pairs={{0,2},{2,0},{1,3},{3,1},{4,6},{6,4},{5,7},{7,5},{8,10},{10,8},{9,1... | collective-permute-start | bytes 2396168 | tf_op jit(solution)/shard_map/ppermute | solution.py:402
  90.6 27.4 %copy-start.6 = (bf16[2,3072]{1,0:T(2,128)(2,1)S(1)}, bf16[2,3072]{1,0:T(2,128)(2,1)}, u32[]{:S(2)}) copy-start(bf16[2,3072]{1,0:T(2,128)(2,1)} %gain.3) | copy-start | bytes 36868
  115.7 2.3 collective-permute-start.8
  163.9 3.6 %collective-permute-start.9 = (f32[128,3072]{1,0:T(8,128)}, f32[128,3072]{1,0:T(8,128)S(1)}, u32[]{:S(2)}, u32[]{:S(2)}) collective-permute-start(f32[128,3072]{1,0:T(8,128)} %get-tuple-element.25), channel_id=1, source_target_pairs={{0,1},{1,0},{2,3},{3,2},{4,5},{5,4},{6,7},{7,6},{8,9},{9,8},{10,11... | collective-permute-start | bytes 4718600 | tf_op jit(solution)/shard_map/ppermute | solution.py:401
  167.7 20.2 %collective-permute-start.12 = (bf16[128,3072]{1,0:T(8,128)(2,1)S(1)}, bf16[128,3072]{1,0:T(8,128)(2,1)S(1)}, u32[]{:S(2)}, u32[]{:S(2)}) collective-permute-start(bf16[128,3072]{1,0:T(8,128)(2,1)S(1)} %add_convert_fusion.1.refs_0_.xa), channel_id=1, source_target_pairs={{0,2},{2,0},{1,3},{3,1},{4,6},{6,4},{5,7},{7,5},{8,10},{10,8},{9,1... | collective-permute-start | bytes 2359304 | tf_op jit(solution)/shard_map/ppermute | solution.py:402
  170.0 17.8 %collective-permute-start.10 = (bf16[128,3072]{1,0:T(8,128)(2,1)S(1)}, bf16[128,3072]{1,0:T(8,128)(2,1)S(1)}, u32[]{:S(2)}, u32[]{:S(2)}) collective-permute-start(bf16[128,3072]{1,0:T(8,128)(2,1)S(1)} %add_convert_fusion.1.refs_0_.xa), channel_id=1, source_target_pairs={{0,1},{1,0},{2,3},{3,2},{4,5},{5,4},{6,7},{7,6},{8,9},{9,8},{10,11... | collective-permute-start | bytes 2359304 | tf_op jit(solution)/shard_map/ppermute | solution.py:401
  187.9 9.2 %collective-permute-start.13 = (bf16[128,3072]{1,0:T(8,128)(2,1)S(1)}, bf16[128,3072]{1,0:T(8,128)(2,1)S(1)}, u32[]{:S(2)}, u32[]{:S(2)}) collective-permute-start(bf16[128,3072]{1,0:T(8,128)(2,1)S(1)} %collective-permute-done.12.refs_0_), channel_id=1, source_target_pairs={{0,1},{1,0},{2,3},{3,2},{4,5},{5,4},{6,7},{7,6},{8,9},{9,8},{10,11... | collective-permute-start | bytes 2359304 | tf_op jit(solution)/shard_map/ppermute | solution.py:401
  197.0 6.9 %copy-start.7 = (bf16[2,4,128,384]{3,2,1,0:T(8,128)(2,1)}, bf16[2,4,128,384]{3,2,1,0:T(8,128)(2,1)S(1)}, u32[]{:S(2)}) copy-start(bf16[2,4,128,384]{3,2,1,0:T(8,128)(2,1)S(1)} %get-tuple-element.26.refs_0_) | copy-start | bytes 2359300
  209.7 28.6 %collective-permute-start.15 = (f32[1,520,384]{2,1,0:T(8,128)}, f32[1,520,384]{2,1,0:T(8,128)S(1)}, u32[]{:S(2)}, u32[]{:S(2)}) collective-permute-start(f32[1,520,384]{2,1,0:T(8,128)} %attn.11), channel_id=1, source_target_pairs={{0,2},{2,0},{1,3},{3,1},{4,6},{6,4},{5,7},{7,5},{8,10},{10,8},{9,1... | collective-permute-start | bytes 2396168 | tf_op jit(solution)/shard_map/ppermute | solution.py:402
  223.0 28.6 %collective-permute-start.14 = (f32[1,520,384]{2,1,0:T(8,128)}, f32[1,520,384]{2,1,0:T(8,128)S(1)}, u32[]{:S(2)}, u32[]{:S(2)}) collective-permute-start(f32[1,520,384]{2,1,0:T(8,128)} %attn.10), channel_id=1, source_target_pairs={{0,2},{2,0},{1,3},{3,1},{4,6},{6,4},{5,7},{7,5},{8,10},{10,8},{9,1... | collective-permute-start | bytes 2396168 | tf_op jit(solution)/shard_map/ppermute | solution.py:402
  253.3 3.3 %collective-permute-start.16 = (bf16[2,128,1536]{2,1,0:T(8,128)(2,1)S(1)}, bf16[2,128,1536]{2,1,0:T(8,128)(2,1)S(1)}, u32[]{:S(2)}, u32[]{:S(2)}) collective-permute-start(bf16[2,128,1536]{2,1,0:T(8,128)(2,1)S(1)} %merge.3.a_own), channel_id=1, source_target_pairs={{0,1},{1,0},{2,3},{3,2},{4,5},{5,4},{6,7},{7,6},{8,9},{9,8},{10,11... | collective-permute-start | bytes 2359304 | tf_op jit(solution)/shard_map/ppermute | solution.py:401
  302.6 3.6 %collective-permute-start.17 = (f32[128,3072]{1,0:T(8,128)}, f32[128,3072]{1,0:T(8,128)S(1)}, u32[]{:S(2)}, u32[]{:S(2)}) collective-permute-start(f32[128,3072]{1,0:T(8,128)} %get-tuple-element.32), channel_id=1, source_target_pairs={{0,1},{1,0},{2,3},{3,2},{4,5},{5,4},{6,7},{7,6},{8,9},{9,8},{10,11... | collective-permute-start | bytes 4718600 | tf_op jit(solution)/shard_map/ppermute | solution.py:401
  (9 other events, 26.5 us)
